TPU v7x, 256 devices: a whole 4x4x8 slice. The times are simulated.
256 devices in a mesh: rep: 4 (over x), ep: 64 (over z, y, core).
Axes of the slice: x: 4, y: 4, z: 8, core: 2. Of those that a mesh axis runs over, the one named last changes fastest.
Arguments:
- out_grad: bfloat16 [16384, 2048], P(('rep', 'ep')), may hold values from -3 to 3
- saved_hidden: bfloat16 [16384, 2, 7168], P(('rep', 'ep')), may hold values from -0.59765625 to 0.59765625
- combine: bfloat16 [16384, 2], P(('rep', 'ep')), may hold values from 0.049804688 to 1
- expert_ids: int32 [16384, 2], P(('rep', 'ep')), may hold values from 0 to 7, all different within a row; in each aligned block of 64 rows (0 to 63, 64 to 127, ...) at most 24 rows name the same one
Outputs:
- down_grad: float32 [57344, 2048], P('ep', 'rep')
Inputs may be any that keep to these rules, and one draw needn't show every extreme that they name: `expert_ids`: in each aligned block of 64 rows (the rows of one device), no expert is named by more than 24 slots, a bound that some block reaches; the 2 ids of a row differ; every expert is named somewhere.
All inputs are finite; a program needn't handle non-finite values.
Results may differ from a plain program's by a relative error of at most 0.0042.
Values may be sent and summed in bfloat16 or wider, within the bound.
No kernel may reach another device: no remote copies, remote signals or barrier semaphores. Data moves between devices by JAX's collectives and lax.ppermute only.
A program may use at most 64 MiB of HBM per device.

v0:
```python
import functools

import jax
import jax.numpy as jnp
from jax import lax
from jax.experimental import pallas as pl
from jax.experimental.pallas import tpu as pltpu
from jax.sharding import Mesh, PartitionSpec as P

EXPERTS = 8
CAP = 24
DIRECT = 384
FAR_FIRST = (4, 3, 5, 2, 6, 1, 7)
VMEM = pl.BlockSpec(memory_space=pltpu.VMEM)
SMEM = pl.BlockSpec(memory_space=pltpu.SMEM)
EARLY = ((0, 0, 0), (0, 1, 0), (0, 3, 0), (1, 0, 0), (1, 1, 0), (1, 3, 0))
LATE = ((0, 2, 0), (0, 2, 4), (1, 2, 0), (1, 2, 4))
BLOCKS = (2, 1, 3, 0)


def cost(flops, moved):
    return pl.CostEstimate(flops=flops, bytes_accessed=moved, transcendentals=0)


def place_matrices(ids):
    tokens = ids.shape[1]
    experts = lax.broadcasted_iota(jnp.int32, (EXPERTS, tokens), 0)
    first = (ids[0:1, :] == experts).astype(jnp.float32)
    second = (ids[1:2, :] == experts).astype(jnp.float32)
    before = (
        lax.broadcasted_iota(jnp.int32, (tokens, tokens), 0)
        < lax.broadcasted_iota(jnp.int32, (tokens, tokens), 1)
    ).astype(jnp.float32)
    ahead_first = jnp.dot(first, before, preferred_element_type=jnp.float32)
    ahead_second = jnp.dot(second, before, preferred_element_type=jnp.float32)
    ahead_second = ahead_second + jnp.sum(first, axis=1, keepdims=True)
    place_first = jnp.sum(first * ahead_first, axis=0, keepdims=True).astype(jnp.int32)
    place_second = jnp.sum(second * ahead_second, axis=0, keepdims=True).astype(jnp.int32)
    rows = lax.broadcasted_iota(jnp.int32, (EXPERTS * CAP, tokens), 0)
    return (
        rows == ids[0:1, :] * CAP + place_first,
        rows == ids[1:2, :] * CAP + place_second,
    )


def pack_grad_kernel(at_ref, ids_ref, prob_ref, grad_ref, out_ref):
    first, second = place_matrices(ids_ref[...])
    prob = prob_ref[...].astype(jnp.float32)
    pick = jnp.where(first, prob[0:1, :], 0.0) + jnp.where(second, prob[1:2, :], 0.0)
    pick = pick.astype(jnp.bfloat16)
    cols = grad_ref.shape[1] // 4
    for k in range(4):
        owner = lax.rem(at_ref[0] + BLOCKS[k], 4)
        block = grad_ref[:, pl.ds(pl.multiple_of(owner * cols, cols), cols)]
        packed = jnp.dot(pick, block, preferred_element_type=jnp.float32).astype(jnp.bfloat16)
        out_ref[:, :, k * cols : (k + 1) * cols] = packed.reshape(EXPERTS, CAP, cols)


def pack_hidden_kernel(unit_cols, ids_ref, hidden_ref, out_ref):
    first, second = place_matrices(ids_ref[...])
    first = jnp.where(first, 1.0, 0.0).astype(jnp.bfloat16)
    second = jnp.where(second, 1.0, 0.0).astype(jnp.bfloat16)
    width = out_ref.shape[3]

    def pack(n, carry):
        owner = lax.rem(n, 4) * 2 + lax.div(n, 4)
        cols = pl.ds(pl.multiple_of(owner * unit_cols, 128), width)
        packed = jnp.dot(
            first, hidden_ref[:, 0, cols], preferred_element_type=jnp.float32
        ) + jnp.dot(second, hidden_ref[:, 1, cols], preferred_element_type=jnp.float32)
        out_ref[n] = packed.astype(jnp.bfloat16).reshape(EXPERTS, CAP, width)
        return carry

    lax.fori_loop(0, 8, pack, 0)


def pack_rest_kernel(unit_cols, at_ref, ids_ref, hidden_ref, *out_refs):
    first, second = place_matrices(lax.rem(ids_ref[...] + (EXPERTS - at_ref[1]), EXPERTS))
    first = jnp.where(first, 1.0, 0.0).astype(jnp.bfloat16)
    second = jnp.where(second, 1.0, 0.0).astype(jnp.bfloat16)
    width = out_refs[0].shape[3]
    for d in range(4):

        def pack(flip, carry, d=d):
            owner = lax.rem(at_ref[2] + d, 4) * 2 + lax.rem(at_ref[3] + flip, 2)
            cols = pl.ds(pl.multiple_of(owner * unit_cols + (unit_cols - width), 128), width)
            packed = jnp.dot(
                first, hidden_ref[:, 0, cols], preferred_element_type=jnp.float32
            ) + jnp.dot(second, hidden_ref[:, 1, cols], preferred_element_type=jnp.float32)
            out_refs[d][flip] = packed.astype(jnp.bfloat16).reshape(EXPERTS, CAP, width)
            return carry

        lax.fori_loop(0, 2, pack, 0)


def for_other_core_kernel(*refs):
    *in_refs, out_ref = refs
    for d in range(4):
        out_ref[d] = in_refs[d][...]


def regroup_kernel(*refs):
    ours, theirs, out_refs = refs[:4], refs[4], refs[5:]
    for s in range(EXPERTS):
        for d in range(4):
            out_refs[s][d] = ours[d][s]
            out_refs[s][4 + d] = theirs[d, s]


def put_kernel(pieces, at_ref, *refs):
    piece_refs, (out_ref, sems) = refs[len(refs) - 2 - len(pieces) : -2], refs[-2:]
    block = out_ref.shape[0] // 8
    copies = []
    for n, (flip, d, low) in enumerate(pieces):
        source = lax.rem(at_ref[3] + flip, 2) * 4 + lax.rem(at_ref[2] + (4 - d), 4)
        start = pl.multiple_of(source * block + low * CAP, 4 * CAP)
        rows = out_ref.at[pl.ds(start, piece_refs[n].shape[0])]
        copies.append(pltpu.make_async_copy(piece_refs[n], rows, sems.at[n]))
    for copy in copies:
        copy.start()
    for copy in copies:
        copy.wait()


def sort_rows_kernel(at_ref, *refs):
    *in_refs, out_ref = refs
    for flip in range(2):
        for d in range(4):
            source = lax.rem(at_ref[3] + flip, 2) * 4 + lax.rem(at_ref[2] + (4 - d), 4)
            for s in range(EXPERTS):
                plane = lax.rem(at_ref[1] + (EXPERTS - s), EXPERTS)
                out_ref[source * EXPERTS + plane] = in_refs[s][flip * 4 + d]


def shifted(array, axis, by):
    n = lax.axis_size(axis)
    return lax.ppermute(array, axis, [(i, (i + by) % n) for i in range(n)])


def other_core(array):
    return lax.ppermute(array, "core", [(0, 1), (1, 0)])


def per_device(out_grad, saved_hidden, combine, expert_ids):
    _, model_width = out_grad.shape
    unit_cols = saved_hidden.shape[2] // 8
    rest = unit_cols - DIRECT
    ids_t, prob_t = expert_ids.T, combine.T
    at = jnp.stack([lax.axis_index(name) for name in ("rep", "z", "y", "core")]).astype(jnp.int32)
    exchange = functools.partial(lax.all_to_all, split_axis=0, concat_axis=0, tiled=True)

    send_grad = pl.pallas_call(
        pack_grad_kernel,
        out_shape=jax.ShapeDtypeStruct((EXPERTS, CAP, model_width), jnp.bfloat16),
        in_specs=[SMEM] + [VMEM] * 3,
        out_specs=VMEM,
        cost_estimate=cost(2 * 192 * 64 * 2048, 1 << 20),
    )(at, ids_t, prob_t, out_grad)
    own = exchange(send_grad, "z")

    plane_rows = pl.pallas_call(
        functools.partial(pack_rest_kernel, unit_cols),
        out_shape=[jax.ShapeDtypeStruct((2, EXPERTS, CAP, rest), jnp.bfloat16)] * 4,
        in_specs=[SMEM] + [VMEM] * 2,
        out_specs=[VMEM] * 4,
        cost_estimate=cost(2 * 192 * 128 * rest * 8, 4 << 20),
    )(at, ids_t, saved_hidden)
    plane_rows = [plane_rows[0]] + [shifted(plane_rows[d], "y", d) for d in (1, 2, 3)]
    part = (None, EXPERTS, CAP, rest)
    ours = pl.BlockSpec(part, lambda i: (0, 0, 0, 0))
    theirs = pl.BlockSpec(part, lambda i: (1, 0, 0, 0))
    for_other = pl.pallas_call(
        for_other_core_kernel,
        grid=(1,),
        out_shape=jax.ShapeDtypeStruct((4, EXPERTS, CAP, rest), jnp.bfloat16),
        in_specs=[theirs] * 4,
        out_specs=pl.BlockSpec((4, EXPERTS, CAP, rest), lambda i: (0, 0, 0, 0)),
        cost_estimate=cost(0, 3 << 20),
    )(*plane_rows)
    rest_to = pl.pallas_call(
        regroup_kernel,
        grid=(1,),
        out_shape=[jax.ShapeDtypeStruct((8, CAP, rest), jnp.bfloat16)] * EXPERTS,
        in_specs=[ours] * 4 + [pl.BlockSpec((4, EXPERTS, CAP, rest), lambda i: (0, 0, 0, 0))],
        out_specs=[pl.BlockSpec((8, CAP, rest), lambda i: (0, 0, 0))] * EXPERTS,
        cost_estimate=cost(0, 5 << 20),
    )(*plane_rows, other_core(for_other))

    send_hidden = pl.pallas_call(
        functools.partial(pack_hidden_kernel, unit_cols),
        out_shape=jax.ShapeDtypeStruct((8, EXPERTS, CAP, DIRECT), jnp.bfloat16),
        in_specs=[VMEM] * 2,
        out_specs=VMEM,
        cost_estimate=cost(2 * 192 * 128 * DIRECT * 8, 4 << 20),
    )(ids_t, saved_hidden)
    arrived = exchange(send_hidden.reshape(64, CAP, DIRECT), ("core", "y", "z"))

    half = EXPERTS // 2
    behind, ahead = shifted(own, "y", 1), shifted(own, "y", 3)
    far_low, far_high = shifted(behind[:half], "y", 1), shifted(ahead[half:], "y", 3)
    flat = [piece.reshape(-1, model_width) for piece in (own, behind, ahead, far_low, far_high)]
    theirs = [other_core(piece) for piece in flat]
    rest_from = [rest_to[0]] + [None] * 7
    for s in FAR_FIRST:
        rest_from[s] = shifted(rest_to[s], "z", s)

    cols = model_width // 4
    hbm = pl.BlockSpec(memory_space=pltpu.HBM)
    whole = jax.ShapeDtypeStruct((64 * CAP, model_width), jnp.bfloat16)
    grad_rows = pl.pallas_call(
        functools.partial(put_kernel, EARLY),
        out_shape=whole,
        in_specs=[SMEM] + [VMEM] * len(EARLY),
        out_specs=hbm,
        scratch_shapes=[pltpu.SemaphoreType.DMA((len(EARLY),))],
        cost_estimate=cost(0, 9 << 20),
    )(at, *flat[:3], *theirs[:3])
    grad_rows = pl.pallas_call(
        functools.partial(put_kernel, LATE),
        out_shape=whole,
        in_specs=[SMEM, hbm] + [VMEM] * len(LATE),
        out_specs=hbm,
        scratch_shapes=[pltpu.SemaphoreType.DMA((len(LATE),))],
        input_output_aliases={1: 0},
        cost_estimate=cost(0, 3 << 20),
    )(at, grad_rows, *flat[3:], *theirs[3:])

    def product(hidden, start, stop):
        return lax.dot_general(
            hidden,
            grad_rows[:, start:stop],
            (((0,), (0,)), ((), ())),
            preferred_element_type=jnp.float32,
        )

    def partial_sums(hidden):
        half = hidden.shape[1] // 2
        far = product(hidden, 0, cols).astype(jnp.bfloat16)
        far = [far[:half], far[half:]]
        near = product(hidden, cols, 4 * cols)
        return far, near

    def exchanged(far, near):
        right, left, own_part = (near[:, k * cols : (k + 1) * cols] for k in range(3))
        half = near.shape[0] // 2
        from_left, from_right = shifted(far[0], "rep", 1), shifted(far[1], "rep", 3)
        from_left, from_right = from_left.astype(jnp.float32), from_right.astype(jnp.float32)
        right = (right + jnp.pad(from_left, ((0, half), (0, 0)))).astype(jnp.bfloat16)
        left = (left + jnp.pad(from_right, ((half, 0), (0, 0)))).astype(jnp.bfloat16)
        return own_part, shifted(right, "rep", 1), shifted(left, "rep", 3)

    def summed(own_part, from_left, from_right):
        return own_part + from_left.astype(jnp.float32) + from_right.astype(jnp.float32)

    direct = exchanged(*partial_sums(arrived.reshape(-1, DIRECT)))
    rest_rows = pl.pallas_call(
        sort_rows_kernel,
        out_shape=jax.ShapeDtypeStruct((64, CAP, rest), jnp.bfloat16),
        in_specs=[SMEM] + [VMEM] * EXPERTS,
        out_specs=VMEM,
        cost_estimate=cost(0, 3 << 20),
    )(at, *rest_from)
    other = exchanged(*partial_sums(rest_rows.reshape(-1, rest)))
    return jnp.concatenate([summed(*direct), summed(*other)], axis=0)


def solution(mesh):
    wide = Mesh(mesh.devices.reshape(4, 8, 4, 2), ("rep", "z", "y", "core"))
    rows = ("rep", "z", "y", "core")
    in_specs = (P(rows, None), P(rows, None, None), P(rows, None), P(rows, None))
    out_specs = P(("z", "y", "core"), "rep")
    return jax.shard_map(
        per_device, mesh=wide, in_specs=in_specs, out_specs=out_specs, check_vma=False
    )
```

profile of v0, /device:TPU:40, one launch (start us, length us, event | category | flops | bytes accessed | tf_op | source)
XLA Modules:
  0.0 181.3 jit_solution(15883156077307198758)
XLA Ops:
  0.6 2.3 %shard_map.47 = bf16[8,24,2048]{2,1,0:T(8,128)(2,1)} custom-call(s32[4]{0:T(128)} %pad_add_fusion.at_ref, s32[2,64]{1,0:T(2,128)} %bitcast.29, bf16[2,64]{1,0:T(2,128)(2,1)} %bitcast.32, bf16[64,2048]{1,0:T(8,128)(2,1)} %grad_ref.1), custom_call_target="tpu_custom_call" | custom-call | flops 50331648 | bytes 1048576 | tf_op jit(solution)/shard_map/pallas_call | solution.py:152
  3.0 8.6 %all-to-all-start.1 = ((bf16[8,24,2048]{2,1,0:T(8,128)(2,1)}), bf16[8,24,2048]{2,1,0:T(8,128)(2,1)S(1)}, u32[]{:S(2)}, u32[]{:S(2)}) async-start(bf16[8,24,2048]{2,1,0:T(8,128)(2,1)} %shard_map.47), calls=%async_computation.1 | async-start | bytes 1572864 | tf_op jit(solution)/shard_map/all_to_all | solution.py:159
  11.5 6.1 %shard_map.50 = (bf16[2,8,24,512]{3,2,1,0:T(8,128)(2,1)}, bf16[2,8,24,512]{3,2,1,0:T(8,128)(2,1)}, bf16[2,8,24,512]{3,2,1,0:T(8,128)(2,1)}, bf16[2,8,24,512]{3,2,1,0:T(8,128)(2,1)}) custom-call(s32[4]{0:T(128)} %pad_add_fusion.at_ref, s32[2,64]{1,0:T(2,128)} %bitcast.30, bf16[64,2,7168]{2,1,0:T(2,128)(2,1)} %hidden_ref.3), custom_call_target="tpu_custom_call" | custom-call | flops 201326592 | bytes 4194304 | tf_op jit(solution)/shard_map/pallas_call | solution.py:161
  17.6 1.6 collective-permute-start.13
  19.2 0.9 collective-permute-start.14
  20.1 2.4 %collective-permute-start.15 = (bf16[2,8,24,512]{3,2,1,0:T(8,128)(2,1)}, bf16[2,8,24,512]{3,2,1,0:T(8,128)(2,1)S(1)}, u32[]{:S(2)}, u32[]{:S(2)}) collective-permute-start(bf16[2,8,24,512]{3,2,1,0:T(8,128)(2,1)} %get-tuple-element.20), channel_id=1, source_target_pairs={{0,6},{2,0},{4,2},{6,4},{1,7},{3,1},{5,3},{7,5},{8,14},{10,8},{12,... | collective-permute-start | bytes 1179656 | tf_op jit(solution)/shard_map/ppermute | solution.py:137
  22.6 6.0 %shard_map.46 = bf16[8,8,24,384]{3,2,1,0:T(8,128)(2,1)} custom-call(s32[2,64]{1,0:T(2,128)} %bitcast.31, bf16[64,2,7168]{2,1,0:T(2,128)(2,1)} %hidden_ref.3), custom_call_target="tpu_custom_call" | custom-call | flops 150994944 | bytes 4194304 | tf_op jit(solution)/shard_map/pallas_call | solution.py:189
  28.6 4.6 %all-to-all-done.1 = bf16[8,24,2048]{2,1,0:T(8,128)(2,1)S(1)} async-done(((bf16[8,24,2048]{2,1,0:T(8,128)(2,1)}), bf16[8,24,2048]{2,1,0:T(8,128)(2,1)S(1)}, u32[]{:S(2)}, u32[]{:S(2)}) %all-to-all-start.1) | async-done | bytes 786464 | tf_op jit(solution)/shard_map/all_to_all | solution.py:159
  33.2 6.5 %all-to-all-start = ((bf16[64,24,384]{2,1,0:T(8,128)(2,1)}), bf16[64,24,384]{2,1,0:T(8,128)(2,1)}, u32[]{:S(2)}, u32[]{:S(2)}) async-start(bf16[64,24,384]{2,1,0:T(8,128)(2,1)} %bitcast.18), calls=%async_computation | async-start | bytes 2359296 | tf_op jit(solution)/shard_map/all_to_all | solution.py:196
  39.8 0.7 copy-done.4
  40.8 2.1 %shard_map.51 = bf16[4,8,24,512]{3,2,1,0:T(8,128)(2,1)} custom-call(bf16[2,8,24,512]{3,2,1,0:T(8,128)(2,1)} %get-tuple-element.17.refs_0_, bf16[2,8,24,512]{3,2,1,0:T(8,128)(2,1)} %copy-done.4, bf16[2,8,24,512]{3,2,1,0:T(8,128)(2,1)} %copy-done.5, bf16[2,8,24,512]{3,2,1,0:T(8,128)(2,1)} %copy-done.6), custom_call_target="tpu_custom_call" | custom-call | bytes 3145728 | tf_op jit(solution)/shard_map/pallas_call | solution.py:172
  43.2 1.5 collective-permute-start
  45.4 0.9 copy-done.8
  46.3 2.7 %shard_map.52 = (bf16[8,24,512]{2,1,0:T(8,128)(2,1)}, bf16[8,24,512]{2,1,0:T(8,128)(2,1)}, bf16[8,24,512]{2,1,0:T(8,128)(2,1)}, bf16[8,24,512]{2,1,0:T(8,128)(2,...) custom-call(bf16[2,8,24,512]{3,2,1,0:T(8,128)(2,1)} %get-tuple-eleme, ...), custom_call_target="tpu_custom_call" | custom-call | bytes 5242880 | tf_op jit(solution)/shard_map/pallas_call | solution.py:180
  49.0 1.5 collective-permute-start.17
  50.5 3.6 %collective-permute-start.18 = (bf16[8,24,512]{2,1,0:T(8,128)(2,1)}, bf16[8,24,512]{2,1,0:T(8,128)(2,1)S(1)}, u32[]{:S(2)}, u32[]{:S(2)}) collective-permute-start(bf16[8,24,512]{2,1,0:T(8,128)(2,1)} %get-tuple-element.23), channel_id=1, source_target_pairs={{0,16},{8,24},{16,32},{24,40},{32,48},{40,56},{48,0},{56,8},{1,17}... | collective-permute-start | bytes 589832 | tf_op jit(solution)/shard_map/ppermute | solution.py:137
  54.6 16.4 %collective-permute-done.17.refs_1_ = bf16[8,24,512]{2,1,0:T(8,128)(2,1)S(1)} collective-permute-done((bf16[8,24,512]{2,1,0:T(8,128)(2,1)}, bf16[8,24,512]{2,1,0:T(8,128)(2,1)S(1)}, u32[]{:S(2)}, u32[]{:S(2)}) %collective-permute-start.17) | collective-permute-done | bytes 196640 | tf_op jit(solution)/shard_map/ppermute | solution.py:137
  71.0 5.2 %collective-permute-start.20 = (bf16[8,24,512]{2,1,0:T(8,128)(2,1)}, bf16[8,24,512]{2,1,0:T(8,128)(2,1)S(1)}, u32[]{:S(2)}, u32[]{:S(2)}) collective-permute-start(bf16[8,24,512]{2,1,0:T(8,128)(2,1)} %get-tuple-element.25), channel_id=1, source_target_pairs={{0,32},{8,40},{16,48},{24,56},{32,0},{40,8},{48,16},{56,24},{1,33}... | collective-permute-start | bytes 589832 | tf_op jit(solution)/shard_map/ppermute | solution.py:137
  76.2 6.2 %collective-permute-done.18.refs_2_ = bf16[8,24,512]{2,1,0:T(8,128)(2,1)S(1)} collective-permute-done((bf16[8,24,512]{2,1,0:T(8,128)(2,1)}, bf16[8,24,512]{2,1,0:T(8,128)(2,1)S(1)}, u32[]{:S(2)}, u32[]{:S(2)}) %collective-permute-start.18) | collective-permute-done | bytes 196640 | tf_op jit(solution)/shard_map/ppermute | solution.py:137
  82.3 4.7 %collective-permute-start.21 = (bf16[8,24,512]{2,1,0:T(8,128)(2,1)}, bf16[8,24,512]{2,1,0:T(8,128)(2,1)S(1)}, u32[]{:S(2)}, u32[]{:S(2)}) collective-permute-start(bf16[8,24,512]{2,1,0:T(8,128)(2,1)} %get-tuple-element.26), channel_id=1, source_target_pairs={{0,40},{8,48},{16,56},{24,0},{32,8},{40,16},{48,24},{56,32},{1,41}... | collective-permute-start | bytes 589832 | tf_op jit(solution)/shard_map/ppermute | solution.py:137
  87.0 0.9 collective-permute-start.22
  88.3 4.1 %collective-permute-done.19.refs_3_ = bf16[8,24,512]{2,1,0:T(8,128)(2,1)S(1)} collective-permute-done((bf16[8,24,512]{2,1,0:T(8,128)(2,1)}, bf16[8,24,512]{2,1,0:T(8,128)(2,1)S(1)}, u32[]{:S(2)}, u32[]{:S(2)}) %collective-permute-start.19) | collective-permute-done | bytes 196640 | tf_op jit(solution)/shard_map/ppermute | solution.py:137
  92.9 11.0 %collective-permute-done.21.refs_5_ = bf16[8,24,512]{2,1,0:T(8,128)(2,1)S(1)} collective-permute-done((bf16[8,24,512]{2,1,0:T(8,128)(2,1)}, bf16[8,24,512]{2,1,0:T(8,128)(2,1)S(1)}, u32[]{:S(2)}, u32[]{:S(2)}) %collective-permute-start.21) | collective-permute-done | bytes 196640 | tf_op jit(solution)/shard_map/ppermute | solution.py:137
  103.9 1.5 collective-permute-start.5
  105.4 1.1 collective-permute-done.22.refs_6_
  106.5 4.4 %collective-permute-done.23.refs_7_ = bf16[8,24,512]{2,1,0:T(8,128)(2,1)S(1)} collective-permute-done((bf16[8,24,512]{2,1,0:T(8,128)(2,1)}, bf16[8,24,512]{2,1,0:T(8,128)(2,1)S(1)}, u32[]{:S(2)}, u32[]{:S(2)}) %collective-permute-start.23) | collective-permute-done | bytes 196640 | tf_op jit(solution)/shard_map/ppermute | solution.py:137
  110.9 0.8 collective-permute-start.6
  111.7 2.4 %collective-permute-done.5 = bf16[4,24,2048]{2,1,0:T(8,128)(2,1)S(1)} collective-permute-done((bf16[4,24,2048]{2,1,0:T(8,128)(2,1)S(1)}, bf16[4,24,2048]{2,1,0:T(8,128)(2,1)S(1)}, u32[]{:S(2)}, u32[]{:S(2)}) %collective-permute-start.5) | collective-permute-done | bytes 393248 | tf_op jit(solution)/shard_map/ppermute | solution.py:137
  114.1 7.6 %collective-permute-done.6 = bf16[4,24,2048]{2,1,0:T(8,128)(2,1)} collective-permute-done((bf16[4,24,2048]{2,1,0:T(8,128)(2,1)S(1)}, bf16[4,24,2048]{2,1,0:T(8,128)(2,1)}, u32[]{:S(2)}, u32[]{:S(2)}) %collective-permute-start.6) | collective-permute-done | bytes 393248 | tf_op jit(solution)/shard_map/ppermute | solution.py:137
  121.7 2.8 %shard_map.53 = bf16[64,24,512]{2,1,0:T(8,128)(2,1)} custom-call(s32[4]{0:T(128)} %pad_add_fusion.at_ref, bf16[8,24,512]{2,1,0:T(8,128)(2,1)} %get-tuple-element.21.refs_0_, bf16[8,24,512]{2,1,0:T(8,128)(2,1)} %copy-done.11, bf16[8,24,512]{2,1,0:T(8,128)(2,1)} %copy-done.12, bf16[8,24,512]{2,1,0:T(8,128)(2,1)} %copy-done.13, bf16[8,24,512]{2,1,0:T(8,128)(2,1)} %copy-done.14, ...), custom_call_target="tpu_custom_call" | custom-call | bytes 3145728 | tf_op jit(solution)/shard_map/pallas_call | solution.py:256
  124.5 0.8 copy-done.9
  125.4 4.5 %shard_map.48.refs_0_ = bf16[1536,2048]{1,0:T(8,128)(2,1)} custom-call(s32[4]{0:T(128)} %pad_add_fusion.at_ref, bf16[192,2048]{1,0:T(8,128)(2,1)} %bitcast.20, bf16[192,2048]{1,0:T(8,128)(2,1)} %bitcast.22, bf16[192,2048]{1,0:T(8,128)(2,1)} %bitcast.24, bf16[192,2048]{1,0:T(8,128)(2,1)} %copy-done.9, bf16[192,2048]{1,0:T(8,128)(2,1)} %collective-permute-done.3.refs_4_, ...), custom_call_target="tpu_custom_call" | custom-call | bytes 9437184 | tf_op jit(solution)/shard_map/pallas_call | solution.py:210
  130.0 2.6 %shard_map.49 = bf16[1536,2048]{1,0:T(8,128)(2,1)} custom-call(s32[4]{0:T(128)} %pad_add_fusion.at_ref, bf16[1536,2048]{1,0:T(8,128)(2,1)} %shard_map.48.refs_0_, bf16[96,2048]{1,0:T(8,128)(2,1)} %bitcast.28, bf16[96,2048]{1,0:T(8,128)(2,1)} %bitcast.12.refs_2_, bf16[96,2048]{1,0:T(8,128)(2,1)} %collective-permute-done.7.refs_3_, ...), custom_call_target="tpu_custom_call", output_to_operand_aliasing={{}: (1, {})} | custom-call | bytes 3145728 | tf_op jit(solution)/shard_map/pallas_call | solution.py:218
  132.6 4.9 %fusion.2 = f32[384,1536]{1,0:T(8,128)S(1)} fusion(bf16[1536,384]{1,0:T(8,128)(2,1)} %bitcast.2, bf16[1536,2048]{1,0:T(8,128)(2,1)} %shard_map.49), kind=kOutput, calls=%fused_computation.2 | convolution fusion | flops 1811939328 | bytes 8257536 | tf_op jit(solution)/shard_map/dot_general | solution.py:229
  137.5 2.2 %fusion.11 = bf16[384,512]{1,0:T(8,128)(2,1)S(1)} fusion(bf16[1536,384]{1,0:T(8,128)(2,1)} %bitcast.2, bf16[1536,2048]{1,0:T(8,128)(2,1)S(1)} %copy-done), kind=kOutput, calls=%fused_computation.10 | convolution fusion | flops 604176384 | bytes 3145728 | tf_op jit(solution)/shard_map/dot_general | solution.py:229
  139.7 1.0 fusion.8
  140.7 2.7 %fusion = f32[512,1536]{1,0:T(8,128)S(1)} fusion(bf16[1536,512]{1,0:T(8,128)(2,1)S(1)} %bitcast.26, bf16[1536,2048]{1,0:T(8,128)(2,1)S(1)} %copy-done), kind=kOutput, calls=%fused_computation | convolution fusion | flops 2415919104 | bytes 9437184 | tf_op jit(solution)/shard_map/dot_general | solution.py:229
  143.4 2.8 %collective-permute-start.11 = (bf16[192,512]{1,0:T(8,128)(2,1)S(1)}, bf16[192,512]{1,0:T(8,128)(2,1)S(1)}, u32[]{:S(2)}, u32[]{:S(2)}) collective-permute-start(bf16[192,512]{1,0:T(8,128)(2,1)S(1)} %get-tuple-element.36), channel_id=1, source_target_pairs={{0,192},{64,0},{128,64},{192,128},{1,193},{65,1},{129,65},{193,129... | collective-permute-start | bytes 589832 | tf_op jit(solution)/shard_map/ppermute | solution.py:137
  146.3 1.1 collective-permute-start.24
  147.4 2.6 %collective-permute-start.26 = (bf16[256,512]{1,0:T(8,128)(2,1)S(1)}, bf16[256,512]{1,0:T(8,128)(2,1)S(1)}, u32[]{:S(2)}, u32[]{:S(2)}) collective-permute-start(bf16[256,512]{1,0:T(8,128)(2,1)S(1)} %get-tuple-element.34), channel_id=1, source_target_pairs={{0,192},{64,0},{128,64},{192,128},{1,193},{65,1},{129,65},{193,129... | collective-permute-start | bytes 786440 | tf_op jit(solution)/shard_map/ppermute | solution.py:137
  149.9 1.6 collective-permute-done.11
  151.5 3.7 %collective-permute-done.9 = bf16[192,512]{1,0:T(8,128)(2,1)S(1)} collective-permute-done((bf16[192,512]{1,0:T(8,128)(2,1)S(1)}, bf16[192,512]{1,0:T(8,128)(2,1)S(1)}, u32[]{:S(2)}, u32[]{:S(2)}) %collective-permute-start.9) | collective-permute-done | bytes 196640 | tf_op jit(solution)/shard_map/ppermute | solution.py:137
  155.5 3.2 %collective-permute-start.12 = (bf16[384,512]{1,0:T(8,128)(2,1)S(1)}, bf16[384,512]{1,0:T(8,128)(2,1)S(1)}, u32[]{:S(2)}, u32[]{:S(2)}) collective-permute-start(bf16[384,512]{1,0:T(8,128)(2,1)S(1)} %get-tuple-element.32), channel_id=1, source_target_pairs={{0,192},{64,0},{128,64},{192,128},{1,193},{65,1},{129,65},{193,129... | collective-permute-start | bytes 1179656 | tf_op jit(solution)/shard_map/ppermute | solution.py:137
  158.7 2.1 %collective-permute-done.24 = bf16[256,512]{1,0:T(8,128)(2,1)S(1)} collective-permute-done((bf16[256,512]{1,0:T(8,128)(2,1)S(1)}, bf16[256,512]{1,0:T(8,128)(2,1)S(1)}, u32[]{:S(2)}, u32[]{:S(2)}) %collective-permute-start.24) | collective-permute-done | bytes 262176 | tf_op jit(solution)/shard_map/ppermute | solution.py:137
  161.2 3.2 %collective-permute-start.27 = (bf16[512,512]{1,0:T(8,128)(2,1)S(1)}, bf16[512,512]{1,0:T(8,128)(2,1)S(1)}, u32[]{:S(2)}, u32[]{:S(2)}) collective-permute-start(bf16[512,512]{1,0:T(8,128)(2,1)S(1)} %get-tuple-element.30), channel_id=1, source_target_pairs={{0,192},{64,0},{128,64},{192,128},{1,193},{65,1},{129,65},{193,129... | collective-permute-start | bytes 1572872 | tf_op jit(solution)/shard_map/ppermute | solution.py:137
  164.4 4.9 %collective-permute-done.10 = bf16[384,512]{1,0:T(8,128)(2,1)S(1)} collective-permute-done((bf16[384,512]{1,0:T(8,128)(2,1)S(1)}, bf16[384,512]{1,0:T(8,128)(2,1)S(1)}, u32[]{:S(2)}, u32[]{:S(2)}) %collective-permute-start.10) | collective-permute-done | bytes 393248 | tf_op jit(solution)/shard_map/ppermute | solution.py:137
  169.4 10.2 %collective-permute-done.25 = bf16[512,512]{1,0:T(8,128)(2,1)S(1)} collective-permute-done((bf16[512,512]{1,0:T(8,128)(2,1)S(1)}, bf16[512,512]{1,0:T(8,128)(2,1)S(1)}, u32[]{:S(2)}, u32[]{:S(2)}) %collective-permute-start.25) | collective-permute-done | bytes 524320 | tf_op jit(solution)/shard_map/ppermute | solution.py:137
  179.9 1.4 pad_maximum_fusion
  (70 shorter events, 4.4 us)
Async XLA Ops:
  3.0 30.2 %all-to-all-start.1 = ((bf16[8,24,2048]{2,1,0:T(8,128)(2,1)}), bf16[8,24,2048]{2,1,0:T(8,128)(2,1)S(1)}, u32[]{:S(2)}, u32[]{:S(2)}) async-start(bf16[8,24,2048]{2,1,0:T(8,128)(2,1)} %shard_map.47), calls=%async_computation.1 | async-start | bytes 1572864 | tf_op jit(solution)/shard_map/all_to_all | solution.py:159
  17.6 22.1 %collective-permute-start.13 = (bf16[2,8,24,512]{3,2,1,0:T(8,128)(2,1)}, bf16[2,8,24,512]{3,2,1,0:T(8,128)(2,1)S(1)}, u32[]{:S(2)}, u32[]{:S(2)}) collective-permute-start(bf16[2,8,24,512]{3,2,1,0:T(8,128)(2,1)} %get-tuple-element.18), channel_id=1, source_target_pairs={{0,2},{2,4},{4,6},{6,0},{1,3},{3,5},{5,7},{7,1},{8,10},{10,12},{12... | collective-permute-start | bytes 1179656 | tf_op jit(solution)/shard_map/ppermute | solution.py:137
  19.2 20.6 %collective-permute-start.14 = (bf16[2,8,24,512]{3,2,1,0:T(8,128)(2,1)}, bf16[2,8,24,512]{3,2,1,0:T(8,128)(2,1)S(1)}, u32[]{:S(2)}, u32[]{:S(2)}) collective-permute-start(bf16[2,8,24,512]{3,2,1,0:T(8,128)(2,1)} %get-tuple-element.19), channel_id=1, source_target_pairs={{0,4},{2,6},{4,0},{6,2},{1,5},{3,7},{5,1},{7,3},{8,12},{10,14},{12... | collective-permute-start | bytes 1179656 | tf_op jit(solution)/shard_map/ppermute | solution.py:137
  20.1 19.6 %collective-permute-start.15 = (bf16[2,8,24,512]{3,2,1,0:T(8,128)(2,1)}, bf16[2,8,24,512]{3,2,1,0:T(8,128)(2,1)S(1)}, u32[]{:S(2)}, u32[]{:S(2)}) collective-permute-start(bf16[2,8,24,512]{3,2,1,0:T(8,128)(2,1)} %get-tuple-element.20), channel_id=1, source_target_pairs={{0,6},{2,0},{4,2},{6,4},{1,7},{3,1},{5,3},{7,5},{8,14},{10,8},{12,... | collective-permute-start | bytes 1179656 | tf_op jit(solution)/shard_map/ppermute | solution.py:137
  33.2 59.2 %copy-start.1 = (bf16[8,24,2048]{2,1,0:T(8,128)(2,1)}, bf16[8,24,2048]{2,1,0:T(8,128)(2,1)S(1)}, u32[]{:S(2)}) copy-start(bf16[8,24,2048]{2,1,0:T(8,128)(2,1)S(1)} %all-to-all-done.1) | copy-start | bytes 2359300
  33.2 99.4 %all-to-all-start = ((bf16[64,24,384]{2,1,0:T(8,128)(2,1)}), bf16[64,24,384]{2,1,0:T(8,128)(2,1)}, u32[]{:S(2)}, u32[]{:S(2)}) async-start(bf16[64,24,384]{2,1,0:T(8,128)(2,1)} %bitcast.18), calls=%async_computation | async-start | bytes 2359296 | tf_op jit(solution)/shard_map/all_to_all | solution.py:196
  39.7 0.8 copy-start.4
  39.8 0.9 copy-start.5
  39.8 1.0 copy-start.6
  42.9 2.5 %collective-permute-start.16 = (bf16[4,8,24,512]{3,2,1,0:T(8,128)(2,1)}, bf16[4,8,24,512]{3,2,1,0:T(8,128)(2,1)S(1)}, u32[]{:S(2)}, u32[]{:S(2)}) collective-permute-start(bf16[4,8,24,512]{3,2,1,0:T(8,128)(2,1)} %shard_map.51), channel_id=1, source_target_pairs={{0,1},{1,0},{2,3},{3,2},{4,5},{5,4},{6,7},{7,6},{8,9},{9,8},{10,11... | collective-permute-start | bytes 2359304 | tf_op jit(solution)/shard_map/ppermute | solution.py:141
  43.2 43.8 %collective-permute-start = (bf16[8,24,2048]{2,1,0:T(8,128)(2,1)S(1)}, bf16[8,24,2048]{2,1,0:T(8,128)(2,1)S(1)}, u32[]{:S(2)}, u32[]{:S(2)}) collective-permute-start(bf16[8,24,2048]{2,1,0:T(8,128)(2,1)S(1)} %all-to-all-done.1), channel_id=1, source_target_pairs={{0,2},{2,4},{4,6},{6,0},{1,3},{3,5},{5,7},{7,1},{8,10},{10,12},{12... | collective-permute-start | bytes 2359304 | tf_op jit(solution)/shard_map/ppermute | solution.py:137
  44.7 43.2 %collective-permute-start.1 = (bf16[8,24,2048]{2,1,0:T(8,128)(2,1)S(1)}, bf16[8,24,2048]{2,1,0:T(8,128)(2,1)S(1)}, u32[]{:S(2)}, u32[]{:S(2)}) collective-permute-start(bf16[8,24,2048]{2,1,0:T(8,128)(2,1)S(1)} %all-to-all-done.1), channel_id=1, source_target_pairs={{0,6},{2,0},{4,2},{6,4},{1,7},{3,1},{5,3},{7,5},{8,14},{10,8},{12,... | collective-permute-start | bytes 2359304 | tf_op jit(solution)/shard_map/ppermute | solution.py:137
  45.4 0.9 copy-start.8
  49.0 22.0 %collective-permute-start.17 = (bf16[8,24,512]{2,1,0:T(8,128)(2,1)}, bf16[8,24,512]{2,1,0:T(8,128)(2,1)S(1)}, u32[]{:S(2)}, u32[]{:S(2)}) collective-permute-start(bf16[8,24,512]{2,1,0:T(8,128)(2,1)} %get-tuple-element.22), channel_id=1, source_target_pairs={{0,8},{8,16},{16,24},{24,32},{32,40},{40,48},{48,56},{56,0},{1,9},... | collective-permute-start | bytes 589832 | tf_op jit(solution)/shard_map/ppermute | solution.py:137
  50.5 31.9 %collective-permute-start.18 = (bf16[8,24,512]{2,1,0:T(8,128)(2,1)}, bf16[8,24,512]{2,1,0:T(8,128)(2,1)S(1)}, u32[]{:S(2)}, u32[]{:S(2)}) collective-permute-start(bf16[8,24,512]{2,1,0:T(8,128)(2,1)} %get-tuple-element.23), channel_id=1, source_target_pairs={{0,16},{8,24},{16,32},{24,40},{32,48},{40,56},{48,0},{56,8},{1,17}... | collective-permute-start | bytes 589832 | tf_op jit(solution)/shard_map/ppermute | solution.py:137
  54.0 38.3 %collective-permute-start.19 = (bf16[8,24,512]{2,1,0:T(8,128)(2,1)}, bf16[8,24,512]{2,1,0:T(8,128)(2,1)S(1)}, u32[]{:S(2)}, u32[]{:S(2)}) collective-permute-start(bf16[8,24,512]{2,1,0:T(8,128)(2,1)} %get-tuple-element.24), channel_id=1, source_target_pairs={{0,24},{8,32},{16,40},{24,48},{32,56},{40,0},{48,8},{56,16},{1,25}... | collective-permute-start | bytes 589832 | tf_op jit(solution)/shard_map/ppermute | solution.py:137
  71.0 16.9 %copy-start.11 = (bf16[8,24,512]{2,1,0:T(8,128)(2,1)}, bf16[8,24,512]{2,1,0:T(8,128)(2,1)S(1)}, u32[]{:S(2)}) copy-start(bf16[8,24,512]{2,1,0:T(8,128)(2,1)S(1)} %collective-permute-done.17.refs_1_) | copy-start | bytes 589828
  71.0 21.4 %collective-permute-start.20 = (bf16[8,24,512]{2,1,0:T(8,128)(2,1)}, bf16[8,24,512]{2,1,0:T(8,128)(2,1)S(1)}, u32[]{:S(2)}, u32[]{:S(2)}) collective-permute-start(bf16[8,24,512]{2,1,0:T(8,128)(2,1)} %get-tuple-element.25), channel_id=1, source_target_pairs={{0,32},{8,40},{16,48},{24,56},{32,0},{40,8},{48,16},{56,24},{1,33}... | collective-permute-start | bytes 589832 | tf_op jit(solution)/shard_map/ppermute | solution.py:137
  82.3 5.6 %copy-start.12 = (bf16[8,24,512]{2,1,0:T(8,128)(2,1)}, bf16[8,24,512]{2,1,0:T(8,128)(2,1)S(1)}, u32[]{:S(2)}) copy-start(bf16[8,24,512]{2,1,0:T(8,128)(2,1)S(1)} %collective-permute-done.18.refs_2_) | copy-start | bytes 589828
  82.3 21.6 %collective-permute-start.21 = (bf16[8,24,512]{2,1,0:T(8,128)(2,1)}, bf16[8,24,512]{2,1,0:T(8,128)(2,1)S(1)}, u32[]{:S(2)}, u32[]{:S(2)}) collective-permute-start(bf16[8,24,512]{2,1,0:T(8,128)(2,1)} %get-tuple-element.26), channel_id=1, source_target_pairs={{0,40},{8,48},{16,56},{24,0},{32,8},{40,16},{48,24},{56,32},{1,41}... | collective-permute-start | bytes 589832 | tf_op jit(solution)/shard_map/ppermute | solution.py:137
  87.0 37.5 %copy-start.2 = (bf16[8,24,2048]{2,1,0:T(8,128)(2,1)}, bf16[8,24,2048]{2,1,0:T(8,128)(2,1)S(1)}, u32[]{:S(2)}) copy-start(bf16[8,24,2048]{2,1,0:T(8,128)(2,1)S(1)} %collective-permute-done) | copy-start | bytes 2359300
  87.0 19.5 %collective-permute-start.22 = (bf16[8,24,512]{2,1,0:T(8,128)(2,1)}, bf16[8,24,512]{2,1,0:T(8,128)(2,1)S(1)}, u32[]{:S(2)}, u32[]{:S(2)}) collective-permute-start(bf16[8,24,512]{2,1,0:T(8,128)(2,1)} %get-tuple-element.27), channel_id=1, source_target_pairs={{0,48},{8,56},{16,0},{24,8},{32,16},{40,24},{48,32},{56,40},{1,49}... | collective-permute-start | bytes 589832 | tf_op jit(solution)/shard_map/ppermute | solution.py:137
  87.9 36.6 %copy-start.3 = (bf16[8,24,2048]{2,1,0:T(8,128)(2,1)}, bf16[8,24,2048]{2,1,0:T(8,128)(2,1)S(1)}, u32[]{:S(2)}) copy-start(bf16[8,24,2048]{2,1,0:T(8,128)(2,1)S(1)} %collective-permute-done.1) | copy-start | bytes 2359300
  87.9 23.0 %collective-permute-start.23 = (bf16[8,24,512]{2,1,0:T(8,128)(2,1)}, bf16[8,24,512]{2,1,0:T(8,128)(2,1)S(1)}, u32[]{:S(2)}, u32[]{:S(2)}) collective-permute-start(bf16[8,24,512]{2,1,0:T(8,128)(2,1)} %get-tuple-element.28), channel_id=1, source_target_pairs={{0,56},{8,0},{16,8},{24,16},{32,24},{40,32},{48,40},{56,48},{1,57}... | collective-permute-start | bytes 589832 | tf_op jit(solution)/shard_map/ppermute | solution.py:137
  92.4 29.3 %copy-start.13 = (bf16[8,24,512]{2,1,0:T(8,128)(2,1)}, bf16[8,24,512]{2,1,0:T(8,128)(2,1)S(1)}, u32[]{:S(2)}) copy-start(bf16[8,24,512]{2,1,0:T(8,128)(2,1)S(1)} %collective-permute-done.19.refs_3_) | copy-start | bytes 589828
  92.4 32.1 %collective-permute-start.2 = (bf16[192,2048]{1,0:T(8,128)(2,1)S(1)}, bf16[192,2048]{1,0:T(8,128)(2,1)S(1)}, u32[]{:S(2)}, u32[]{:S(2)}) collective-permute-start(bf16[192,2048]{1,0:T(8,128)(2,1)S(1)} %bitcast.19), channel_id=1, source_target_pairs={{0,1},{1,0},{2,3},{3,2},{4,5},{5,4},{6,7},{7,6},{8,9},{9,8},{10,11... | collective-permute-start | bytes 2359304 | tf_op jit(solution)/shard_map/ppermute | solution.py:141
  92.4 29.3 %copy-start.14 = (bf16[8,24,512]{2,1,0:T(8,128)(2,1)}, bf16[8,24,512]{2,1,0:T(8,128)(2,1)S(1)}, u32[]{:S(2)}) copy-start(bf16[8,24,512]{2,1,0:T(8,128)(2,1)S(1)} %collective-permute-done.20.refs_4_) | copy-start | bytes 589828
  92.4 32.1 %collective-permute-start.3 = (bf16[192,2048]{1,0:T(8,128)(2,1)S(1)}, bf16[192,2048]{1,0:T(8,128)(2,1)}, u32[]{:S(2)}, u32[]{:S(2)}) collective-permute-start(bf16[192,2048]{1,0:T(8,128)(2,1)S(1)} %bitcast.21), channel_id=1, source_target_pairs={{0,1},{1,0},{2,3},{3,2},{4,5},{5,4},{6,7},{7,6},{8,9},{9,8},{10,11... | collective-permute-start | bytes 2359304 | tf_op jit(solution)/shard_map/ppermute | solution.py:141
  103.9 17.8 %copy-start.15 = (bf16[8,24,512]{2,1,0:T(8,128)(2,1)}, bf16[8,24,512]{2,1,0:T(8,128)(2,1)S(1)}, u32[]{:S(2)}) copy-start(bf16[8,24,512]{2,1,0:T(8,128)(2,1)S(1)} %collective-permute-done.21.refs_5_) | copy-start | bytes 589828
  103.9 10.2 %collective-permute-start.5 = (bf16[4,24,2048]{2,1,0:T(8,128)(2,1)S(1)}, bf16[4,24,2048]{2,1,0:T(8,128)(2,1)S(1)}, u32[]{:S(2)}, u32[]{:S(2)}) collective-permute-start(bf16[4,24,2048]{2,1,0:T(8,128)(2,1)S(1)} %slice.58), channel_id=1, source_target_pairs={{0,2},{2,4},{4,6},{6,0},{1,3},{3,5},{5,7},{7,1},{8,10},{10,12},{12... | collective-permute-start | bytes 1179656 | tf_op jit(solution)/shard_map/ppermute | solution.py:137
  106.5 15.2 %copy-start.16 = (bf16[8,24,512]{2,1,0:T(8,128)(2,1)}, bf16[8,24,512]{2,1,0:T(8,128)(2,1)S(1)}, u32[]{:S(2)}) copy-start(bf16[8,24,512]{2,1,0:T(8,128)(2,1)S(1)} %collective-permute-done.22.refs_6_) | copy-start | bytes 589828
  106.5 18.0 %collective-permute-start.4 = (bf16[192,2048]{1,0:T(8,128)(2,1)S(1)}, bf16[192,2048]{1,0:T(8,128)(2,1)}, u32[]{:S(2)}, u32[]{:S(2)}) collective-permute-start(bf16[192,2048]{1,0:T(8,128)(2,1)S(1)} %bitcast.23), channel_id=1, source_target_pairs={{0,1},{1,0},{2,3},{3,2},{4,5},{5,4},{6,7},{7,6},{8,9},{9,8},{10,11... | collective-permute-start | bytes 2359304 | tf_op jit(solution)/shard_map/ppermute | solution.py:141
  110.9 10.8 %copy-start.17 = (bf16[8,24,512]{2,1,0:T(8,128)(2,1)}, bf16[8,24,512]{2,1,0:T(8,128)(2,1)S(1)}, u32[]{:S(2)}) copy-start(bf16[8,24,512]{2,1,0:T(8,128)(2,1)S(1)} %collective-permute-done.23.refs_7_) | copy-start | bytes 589828
  110.9 10.8 %collective-permute-start.6 = (bf16[4,24,2048]{2,1,0:T(8,128)(2,1)S(1)}, bf16[4,24,2048]{2,1,0:T(8,128)(2,1)}, u32[]{:S(2)}, u32[]{:S(2)}) collective-permute-start(bf16[4,24,2048]{2,1,0:T(8,128)(2,1)S(1)} %slice.59), channel_id=1, source_target_pairs={{0,6},{2,0},{4,2},{6,4},{1,7},{3,1},{5,3},{7,5},{8,14},{10,8},{12,... | collective-permute-start | bytes 1179656 | tf_op jit(solution)/shard_map/ppermute | solution.py:137
  114.1 15.8 %copy-start.10 = (bf16[4,24,2048]{2,1,0:T(8,128)(2,1)}, bf16[4,24,2048]{2,1,0:T(8,128)(2,1)S(1)}, u32[]{:S(2)}) copy-start(bf16[4,24,2048]{2,1,0:T(8,128)(2,1)S(1)} %collective-permute-done.5) | copy-start | bytes 1179652
  114.1 15.8 %collective-permute-start.7 = (bf16[96,2048]{1,0:T(8,128)(2,1)S(1)}, bf16[96,2048]{1,0:T(8,128)(2,1)}, u32[]{:S(2)}, u32[]{:S(2)}) collective-permute-start(bf16[96,2048]{1,0:T(8,128)(2,1)S(1)} %bitcast.27), channel_id=1, source_target_pairs={{0,1},{1,0},{2,3},{3,2},{4,5},{5,4},{6,7},{7,6},{8,9},{9,8},{10,11... | collective-permute-start | bytes 1179656 | tf_op jit(solution)/shard_map/ppermute | solution.py:141
  121.7 8.3 %collective-permute-start.8 = (bf16[96,2048]{1,0:T(8,128)(2,1)}, bf16[96,2048]{1,0:T(8,128)(2,1)}, u32[]{:S(2)}, u32[]{:S(2)}) collective-permute-start(bf16[96,2048]{1,0:T(8,128)(2,1)} %bitcast.12.refs_2_), channel_id=1, source_target_pairs={{0,1},{1,0},{2,3},{3,2},{4,5},{5,4},{6,7},{7,6},{8,9},{9,8},{10,11... | collective-permute-start | bytes 1179656 | tf_op jit(solution)/shard_map/ppermute | solution.py:141
  124.5 0.9 copy-start.9
  132.6 4.9 %copy-start = (bf16[1536,2048]{1,0:T(8,128)(2,1)S(1)}, bf16[1536,2048]{1,0:T(8,128)(2,1)}, u32[]{:S(2)}) copy-start(bf16[1536,2048]{1,0:T(8,128)(2,1)} %shard_map.49) | copy-start | bytes 18874372
  137.5 2.2 %copy-start.7 = (bf16[64,24,512]{2,1,0:T(8,128)(2,1)S(1)}, bf16[64,24,512]{2,1,0:T(8,128)(2,1)}, u32[]{:S(2)}) copy-start(bf16[64,24,512]{2,1,0:T(8,128)(2,1)} %shard_map.53) | copy-start | bytes 4718596
  143.4 8.1 %collective-permute-start.11 = (bf16[192,512]{1,0:T(8,128)(2,1)S(1)}, bf16[192,512]{1,0:T(8,128)(2,1)S(1)}, u32[]{:S(2)}, u32[]{:S(2)}) collective-permute-start(bf16[192,512]{1,0:T(8,128)(2,1)S(1)} %get-tuple-element.36), channel_id=1, source_target_pairs={{0,192},{64,0},{128,64},{192,128},{1,193},{65,1},{129,65},{193,129... | collective-permute-start | bytes 589832 | tf_op jit(solution)/shard_map/ppermute | solution.py:137
  146.2 9.0 %collective-permute-start.9 = (bf16[192,512]{1,0:T(8,128)(2,1)S(1)}, bf16[192,512]{1,0:T(8,128)(2,1)S(1)}, u32[]{:S(2)}, u32[]{:S(2)}) collective-permute-start(bf16[192,512]{1,0:T(8,128)(2,1)S(1)} %get-tuple-element.35), channel_id=1, source_target_pairs={{0,64},{64,128},{128,192},{192,0},{1,65},{65,129},{129,193},{193,1... | collective-permute-start | bytes 589832 | tf_op jit(solution)/shard_map/ppermute | solution.py:137
  146.3 14.6 %collective-permute-start.24 = (bf16[256,512]{1,0:T(8,128)(2,1)S(1)}, bf16[256,512]{1,0:T(8,128)(2,1)S(1)}, u32[]{:S(2)}, u32[]{:S(2)}) collective-permute-start(bf16[256,512]{1,0:T(8,128)(2,1)S(1)} %get-tuple-element.33), channel_id=1, source_target_pairs={{0,64},{64,128},{128,192},{192,0},{1,65},{65,129},{129,193},{193,1... | collective-permute-start | bytes 786440 | tf_op jit(solution)/shard_map/ppermute | solution.py:137
  147.4 13.5 %collective-permute-start.26 = (bf16[256,512]{1,0:T(8,128)(2,1)S(1)}, bf16[256,512]{1,0:T(8,128)(2,1)S(1)}, u32[]{:S(2)}, u32[]{:S(2)}) collective-permute-start(bf16[256,512]{1,0:T(8,128)(2,1)S(1)} %get-tuple-element.34), channel_id=1, source_target_pairs={{0,192},{64,0},{128,64},{192,128},{1,193},{65,1},{129,65},{193,129... | collective-permute-start | bytes 786440 | tf_op jit(solution)/shard_map/ppermute | solution.py:137
  155.4 13.9 %collective-permute-start.10 = (bf16[384,512]{1,0:T(8,128)(2,1)S(1)}, bf16[384,512]{1,0:T(8,128)(2,1)S(1)}, u32[]{:S(2)}, u32[]{:S(2)}) collective-permute-start(bf16[384,512]{1,0:T(8,128)(2,1)S(1)} %get-tuple-element.31), channel_id=1, source_target_pairs={{0,64},{64,128},{128,192},{192,0},{1,65},{65,129},{129,193},{193,1... | collective-permute-start | bytes 1179656 | tf_op jit(solution)/shard_map/ppermute | solution.py:137
  155.5 13.8 %collective-permute-start.12 = (bf16[384,512]{1,0:T(8,128)(2,1)S(1)}, bf16[384,512]{1,0:T(8,128)(2,1)S(1)}, u32[]{:S(2)}, u32[]{:S(2)}) collective-permute-start(bf16[384,512]{1,0:T(8,128)(2,1)S(1)} %get-tuple-element.32), channel_id=1, source_target_pairs={{0,192},{64,0},{128,64},{192,128},{1,193},{65,1},{129,65},{193,129... | collective-permute-start | bytes 1179656 | tf_op jit(solution)/shard_map/ppermute | solution.py:137
  161.1 18.6 %collective-permute-start.25 = (bf16[512,512]{1,0:T(8,128)(2,1)S(1)}, bf16[512,512]{1,0:T(8,128)(2,1)S(1)}, u32[]{:S(2)}, u32[]{:S(2)}) collective-permute-start(bf16[512,512]{1,0:T(8,128)(2,1)S(1)} %get-tuple-element.29), channel_id=1, source_target_pairs={{0,64},{64,128},{128,192},{192,0},{1,65},{65,129},{129,193},{193,1... | collective-permute-start | bytes 1572872 | tf_op jit(solution)/shard_map/ppermute | solution.py:137
  161.2 18.5 %collective-permute-start.27 = (bf16[512,512]{1,0:T(8,128)(2,1)S(1)}, bf16[512,512]{1,0:T(8,128)(2,1)S(1)}, u32[]{:S(2)}, u32[]{:S(2)}) collective-permute-start(bf16[512,512]{1,0:T(8,128)(2,1)S(1)} %get-tuple-element.30), channel_id=1, source_target_pairs={{0,192},{64,0},{128,64},{192,128},{1,193},{65,1},{129,65},{193,129... | collective-permute-start | bytes 1572872 | tf_op jit(solution)/shard_map/ppermute | solution.py:137
where the time goes:
time: 185 us; the launch traced here: 181 us
  waiting for transfers between devices  80.6 us (44%)
  starting transfers between devices  54.8 us (30%)
  Pallas kernels  29.2 us (16%)
  matrix products  10.7 us (6%)
  local copies, waits for them, and re-layouts  2.88 us (2%)
  other arithmetic  2.81 us (2%)
    ppermute x22, waiting for transfers between devices, shifted(): return lax.ppermute(array, axis, [(i, (i + by) % n) for i in range(n)])  75.8 us
    ppermute x22, starting transfers between devices, shifted(): return lax.ppermute(array, axis, [(i, (i + by) % n) for i in range(n)])  38.9 us
    dot_general x4, matrix products, product(): lax.dot_general(hidden, grad_rows[:, start:stop], (((0,), (0,)), ((), ())...  10.7 us
    all_to_all x1, starting transfers between devices, per_device(): own = exchange(send_grad, 'z')  8.57 us
    all_to_all x1, starting transfers between devices, per_device(): arrived = exchange(send_hidden.reshape(64, CAP, DIRECT), ('core', 'y', 'z'))  6.54 us
    pallas_call x1, Pallas kernels, per_device(): pl.pallas_call(functools.partial(pack_rest_kernel, unit_cols), out_shape=...  6.09 us
    pallas_call x1, Pallas kernels, per_device(): pl.pallas_call(functools.partial(pack_hidden_kernel, unit_cols), out_shap...  6.02 us
    all_to_all x1, waiting for transfers between devices, per_device(): own = exchange(send_grad, 'z')  4.61 us
  transfers between devices with their start and end apart: 30, of which 15 were waited for; matrix products, arithmetic and copies ran while one was open for 0% of the time, Pallas kernels for 15%

commit v1 on v0

--- a/solution.py
+++ b/solution.py
@@ -43,14 +43,14 @@
     )
 
 
-def pack_grad_kernel(at_ref, ids_ref, prob_ref, grad_ref, out_ref):
+def pack_grad_kernel(ids_ref, prob_ref, grad_ref, out_ref):
     first, second = place_matrices(ids_ref[...])
     prob = prob_ref[...].astype(jnp.float32)
     pick = jnp.where(first, prob[0:1, :], 0.0) + jnp.where(second, prob[1:2, :], 0.0)
     pick = pick.astype(jnp.bfloat16)
     cols = grad_ref.shape[1] // 4
     for k in range(4):
-        owner = lax.rem(at_ref[0] + BLOCKS[k], 4)
+        owner = lax.rem(lax.axis_index("rep") + BLOCKS[k], 4)
         block = grad_ref[:, pl.ds(pl.multiple_of(owner * cols, cols), cols)]
         packed = jnp.dot(pick, block, preferred_element_type=jnp.float32).astype(jnp.bfloat16)
         out_ref[:, :, k * cols : (k + 1) * cols] = packed.reshape(EXPERTS, CAP, cols)
@@ -152,10 +152,10 @@
     send_grad = pl.pallas_call(
         pack_grad_kernel,
         out_shape=jax.ShapeDtypeStruct((EXPERTS, CAP, model_width), jnp.bfloat16),
-        in_specs=[SMEM] + [VMEM] * 3,
+        in_specs=[VMEM] * 3,
         out_specs=VMEM,
         cost_estimate=cost(2 * 192 * 64 * 2048, 1 << 20),
-    )(at, ids_t, prob_t, out_grad)
+    )(ids_t, prob_t, out_grad)
     own = exchange(send_grad, "z")
 
     plane_rows = pl.pallas_call(
@@ -196,7 +196,8 @@
     arrived = exchange(send_hidden.reshape(64, CAP, DIRECT), ("core", "y", "z"))
 
     half = EXPERTS // 2
-    behind, ahead = shifted(own, "y", 1), shifted(own, "y", 3)
+    behind = shifted(own, "y", 1)
+    ahead = shifted(own, "y", 3)
     far_low, far_high = shifted(behind[:half], "y", 1), shifted(ahead[half:], "y", 3)
     flat = [piece.reshape(-1, model_width) for piece in (own, behind, ahead, far_low, far_high)]
     theirs = [other_core(piece) for piece in flat]
@@ -261,7 +262,8 @@
         cost_estimate=cost(0, 3 << 20),
     )(at, *rest_from)
     other = exchanged(*partial_sums(rest_rows.reshape(-1, rest)))
-    return jnp.concatenate([summed(*direct), summed(*other)], axis=0)
+    first_rows = jnp.pad(summed(*direct), ((0, rest), (0, 0)))
+    return lax.dynamic_update_slice(first_rows, summed(*other), (DIRECT, 0))
 
 
 def solution(mesh):

time: 185 us -> 184 us (level)
  transfers between devices with their start and end apart: 30 -> 30, of which waited for: 15 -> 15; matrix products, arithmetic and copies ran while one was open for 0% -> 1% of each run, Pallas kernels for 15% -> 15%
where the time goes in v1:
time: 184 us; the launch traced here: 181 us
  waiting for transfers between devices  80 us (43%)
  starting transfers between devices  54.8 us (30%)
  Pallas kernels  29.2 us (16%)
  matrix products  10.7 us (6%)
  local copies, waits for them, and re-layouts  2.88 us (2%)
  other arithmetic  2.81 us (2%)
    ppermute x22, waiting for transfers between devices, shifted(): return lax.ppermute(array, axis, [(i, (i + by) % n) for i in range(n)])  75.7 us
    ppermute x22, starting transfers between devices, shifted(): return lax.ppermute(array, axis, [(i, (i + by) % n) for i in range(n)])  38.9 us
    dot_general x4, matrix products, product(): lax.dot_general(hidden, grad_rows[:, start:stop], (((0,), (0,)), ((), ())...  10.7 us
    all_to_all x1, starting transfers between devices, per_device(): own = exchange(send_grad, 'z')  8.57 us
    all_to_all x1, starting transfers between devices, per_device(): arrived = exchange(send_hidden.reshape(64, CAP, DIRECT), ('core', 'y', 'z'))  6.55 us
    pallas_call x1, Pallas kernels, per_device(): pl.pallas_call(functools.partial(pack_rest_kernel, unit_cols), out_shape=...  6.1 us
    pallas_call x1, Pallas kernels, per_device(): pl.pallas_call(functools.partial(pack_hidden_kernel, unit_cols), out_shap...  6.02 us
    pallas_call x1, Pallas kernels, per_device(): pl.pallas_call(functools.partial(put_kernel, EARLY), out_shape=whole, in_...  4.54 us
  transfers between devices with their start and end apart: 30, of which 15 were waited for; matrix products, arithmetic and copies ran while one was open for 1% of the time, Pallas kernels for 15%

profile of v1, /device:TPU:40, one launch (start us, length us, event | category | flops | bytes accessed | tf_op | source)
XLA Modules:
  0.0 180.7 jit_solution(9706046028063585676)
XLA Ops:
  0.0 2.3 %shard_map.47 = bf16[8,24,2048]{2,1,0:T(8,128)(2,1)} custom-call(s32[2,64]{1,0:T(2,128)} %bitcast.29, bf16[2,64]{1,0:T(2,128)(2,1)} %bitcast.32, bf16[64,2048]{1,0:T(8,128)(2,1)} %grad_ref.1), custom_call_target="tpu_custom_call" | custom-call | flops 50331648 | bytes 1048576 | tf_op jit(solution)/shard_map/pallas_call | solution.py:152
  2.3 8.6 %all-to-all-start.1 = ((bf16[8,24,2048]{2,1,0:T(8,128)(2,1)}), bf16[8,24,2048]{2,1,0:T(8,128)(2,1)S(1)}, u32[]{:S(2)}, u32[]{:S(2)}) async-start(bf16[8,24,2048]{2,1,0:T(8,128)(2,1)} %shard_map.47), calls=%async_computation.1 | async-start | bytes 1572864 | tf_op jit(solution)/shard_map/all_to_all | solution.py:159
  11.5 6.1 %shard_map.50 = (bf16[2,8,24,512]{3,2,1,0:T(8,128)(2,1)}, bf16[2,8,24,512]{3,2,1,0:T(8,128)(2,1)}, bf16[2,8,24,512]{3,2,1,0:T(8,128)(2,1)}, bf16[2,8,24,512]{3,2,1,0:T(8,128)(2,1)}) custom-call(s32[4]{0:T(128)} %pad_add_fusion.at_ref, s32[2,64]{1,0:T(2,128)} %bitcast.30, bf16[64,2,7168]{2,1,0:T(2,128)(2,1)} %hidden_ref.3), custom_call_target="tpu_custom_call" | custom-call | flops 201326592 | bytes 4194304 | tf_op jit(solution)/shard_map/pallas_call | solution.py:161
  17.6 1.6 collective-permute-start.13
  19.2 0.9 collective-permute-start.14
  20.1 2.4 %collective-permute-start.15 = (bf16[2,8,24,512]{3,2,1,0:T(8,128)(2,1)}, bf16[2,8,24,512]{3,2,1,0:T(8,128)(2,1)S(1)}, u32[]{:S(2)}, u32[]{:S(2)}) collective-permute-start(bf16[2,8,24,512]{3,2,1,0:T(8,128)(2,1)} %get-tuple-element.20), channel_id=1, source_target_pairs={{0,6},{2,0},{4,2},{6,4},{1,7},{3,1},{5,3},{7,5},{8,14},{10,8},{12,... | collective-permute-start | bytes 1179656 | tf_op jit(solution)/shard_map/ppermute | solution.py:137
  22.5 6.0 %shard_map.46 = bf16[8,8,24,384]{3,2,1,0:T(8,128)(2,1)} custom-call(s32[2,64]{1,0:T(2,128)} %bitcast.31, bf16[64,2,7168]{2,1,0:T(2,128)(2,1)} %hidden_ref.3), custom_call_target="tpu_custom_call" | custom-call | flops 150994944 | bytes 4194304 | tf_op jit(solution)/shard_map/pallas_call | solution.py:189
  28.6 4.0 %all-to-all-done.1 = bf16[8,24,2048]{2,1,0:T(8,128)(2,1)S(1)} async-done(((bf16[8,24,2048]{2,1,0:T(8,128)(2,1)}), bf16[8,24,2048]{2,1,0:T(8,128)(2,1)S(1)}, u32[]{:S(2)}, u32[]{:S(2)}) %all-to-all-start.1) | async-done | bytes 786464 | tf_op jit(solution)/shard_map/all_to_all | solution.py:159
  32.6 6.5 %all-to-all-start = ((bf16[64,24,384]{2,1,0:T(8,128)(2,1)}), bf16[64,24,384]{2,1,0:T(8,128)(2,1)}, u32[]{:S(2)}, u32[]{:S(2)}) async-start(bf16[64,24,384]{2,1,0:T(8,128)(2,1)} %bitcast.18), calls=%async_computation | async-start | bytes 2359296 | tf_op jit(solution)/shard_map/all_to_all | solution.py:196
  39.2 0.7 copy-done.4
  40.2 2.1 %shard_map.51 = bf16[4,8,24,512]{3,2,1,0:T(8,128)(2,1)} custom-call(bf16[2,8,24,512]{3,2,1,0:T(8,128)(2,1)} %get-tuple-element.17.refs_0_, bf16[2,8,24,512]{3,2,1,0:T(8,128)(2,1)} %copy-done.4, bf16[2,8,24,512]{3,2,1,0:T(8,128)(2,1)} %copy-done.5, bf16[2,8,24,512]{3,2,1,0:T(8,128)(2,1)} %copy-done.6), custom_call_target="tpu_custom_call" | custom-call | bytes 3145728 | tf_op jit(solution)/shard_map/pallas_call | solution.py:172
  42.6 1.5 collective-permute-start
  44.8 0.9 copy-done.8
  45.7 2.7 %shard_map.52 = (bf16[8,24,512]{2,1,0:T(8,128)(2,1)}, bf16[8,24,512]{2,1,0:T(8,128)(2,1)}, bf16[8,24,512]{2,1,0:T(8,128)(2,1)}, bf16[8,24,512]{2,1,0:T(8,128)(2,...) custom-call(bf16[2,8,24,512]{3,2,1,0:T(8,128)(2,1)} %get-tuple-eleme, ...), custom_call_target="tpu_custom_call" | custom-call | bytes 5242880 | tf_op jit(solution)/shard_map/pallas_call | solution.py:180
  48.4 1.5 collective-permute-start.17
  49.8 3.6 %collective-permute-start.18 = (bf16[8,24,512]{2,1,0:T(8,128)(2,1)}, bf16[8,24,512]{2,1,0:T(8,128)(2,1)S(1)}, u32[]{:S(2)}, u32[]{:S(2)}) collective-permute-start(bf16[8,24,512]{2,1,0:T(8,128)(2,1)} %get-tuple-element.23), channel_id=1, source_target_pairs={{0,16},{8,24},{16,32},{24,40},{32,48},{40,56},{48,0},{56,8},{1,17}... | collective-permute-start | bytes 589832 | tf_op jit(solution)/shard_map/ppermute | solution.py:137
  54.0 16.4 %collective-permute-done.17.refs_1_ = bf16[8,24,512]{2,1,0:T(8,128)(2,1)S(1)} collective-permute-done((bf16[8,24,512]{2,1,0:T(8,128)(2,1)}, bf16[8,24,512]{2,1,0:T(8,128)(2,1)S(1)}, u32[]{:S(2)}, u32[]{:S(2)}) %collective-permute-start.17) | collective-permute-done | bytes 196640 | tf_op jit(solution)/shard_map/ppermute | solution.py:137
  70.4 5.2 %collective-permute-start.20 = (bf16[8,24,512]{2,1,0:T(8,128)(2,1)}, bf16[8,24,512]{2,1,0:T(8,128)(2,1)S(1)}, u32[]{:S(2)}, u32[]{:S(2)}) collective-permute-start(bf16[8,24,512]{2,1,0:T(8,128)(2,1)} %get-tuple-element.25), channel_id=1, source_target_pairs={{0,32},{8,40},{16,48},{24,56},{32,0},{40,8},{48,16},{56,24},{1,33}... | collective-permute-start | bytes 589832 | tf_op jit(solution)/shard_map/ppermute | solution.py:137
  75.6 6.2 %collective-permute-done.18.refs_2_ = bf16[8,24,512]{2,1,0:T(8,128)(2,1)S(1)} collective-permute-done((bf16[8,24,512]{2,1,0:T(8,128)(2,1)}, bf16[8,24,512]{2,1,0:T(8,128)(2,1)S(1)}, u32[]{:S(2)}, u32[]{:S(2)}) %collective-permute-start.18) | collective-permute-done | bytes 196640 | tf_op jit(solution)/shard_map/ppermute | solution.py:137
  81.7 4.7 %collective-permute-start.21 = (bf16[8,24,512]{2,1,0:T(8,128)(2,1)}, bf16[8,24,512]{2,1,0:T(8,128)(2,1)S(1)}, u32[]{:S(2)}, u32[]{:S(2)}) collective-permute-start(bf16[8,24,512]{2,1,0:T(8,128)(2,1)} %get-tuple-element.26), channel_id=1, source_target_pairs={{0,40},{8,48},{16,56},{24,0},{32,8},{40,16},{48,24},{56,32},{1,41}... | collective-permute-start | bytes 589832 | tf_op jit(solution)/shard_map/ppermute | solution.py:137
  86.4 0.9 collective-permute-start.22
  87.6 4.1 %collective-permute-done.19.refs_3_ = bf16[8,24,512]{2,1,0:T(8,128)(2,1)S(1)} collective-permute-done((bf16[8,24,512]{2,1,0:T(8,128)(2,1)}, bf16[8,24,512]{2,1,0:T(8,128)(2,1)S(1)}, u32[]{:S(2)}, u32[]{:S(2)}) %collective-permute-start.19) | collective-permute-done | bytes 196640 | tf_op jit(solution)/shard_map/ppermute | solution.py:137
  92.3 11.0 %collective-permute-done.21.refs_5_ = bf16[8,24,512]{2,1,0:T(8,128)(2,1)S(1)} collective-permute-done((bf16[8,24,512]{2,1,0:T(8,128)(2,1)}, bf16[8,24,512]{2,1,0:T(8,128)(2,1)S(1)}, u32[]{:S(2)}, u32[]{:S(2)}) %collective-permute-start.21) | collective-permute-done | bytes 196640 | tf_op jit(solution)/shard_map/ppermute | solution.py:137
  103.3 1.5 collective-permute-start.5
  104.8 1.1 collective-permute-done.22.refs_6_
  105.9 4.4 %collective-permute-done.23.refs_7_ = bf16[8,24,512]{2,1,0:T(8,128)(2,1)S(1)} collective-permute-done((bf16[8,24,512]{2,1,0:T(8,128)(2,1)}, bf16[8,24,512]{2,1,0:T(8,128)(2,1)S(1)}, u32[]{:S(2)}, u32[]{:S(2)}) %collective-permute-start.23) | collective-permute-done | bytes 196640 | tf_op jit(solution)/shard_map/ppermute | solution.py:137
  110.3 0.8 collective-permute-start.6
  111.1 2.4 %collective-permute-done.5 = bf16[4,24,2048]{2,1,0:T(8,128)(2,1)S(1)} collective-permute-done((bf16[4,24,2048]{2,1,0:T(8,128)(2,1)S(1)}, bf16[4,24,2048]{2,1,0:T(8,128)(2,1)S(1)}, u32[]{:S(2)}, u32[]{:S(2)}) %collective-permute-start.5) | collective-permute-done | bytes 393248 | tf_op jit(solution)/shard_map/ppermute | solution.py:137
  113.5 7.6 %collective-permute-done.6 = bf16[4,24,2048]{2,1,0:T(8,128)(2,1)} collective-permute-done((bf16[4,24,2048]{2,1,0:T(8,128)(2,1)S(1)}, bf16[4,24,2048]{2,1,0:T(8,128)(2,1)}, u32[]{:S(2)}, u32[]{:S(2)}) %collective-permute-start.6) | collective-permute-done | bytes 393248 | tf_op jit(solution)/shard_map/ppermute | solution.py:137
  121.1 2.8 %shard_map.53 = bf16[64,24,512]{2,1,0:T(8,128)(2,1)} custom-call(s32[4]{0:T(128)} %pad_add_fusion.at_ref, bf16[8,24,512]{2,1,0:T(8,128)(2,1)} %get-tuple-element.21.refs_0_, bf16[8,24,512]{2,1,0:T(8,128)(2,1)} %copy-done.11, bf16[8,24,512]{2,1,0:T(8,128)(2,1)} %copy-done.12, bf16[8,24,512]{2,1,0:T(8,128)(2,1)} %copy-done.13, bf16[8,24,512]{2,1,0:T(8,128)(2,1)} %copy-done.14, ...), custom_call_target="tpu_custom_call" | custom-call | bytes 3145728 | tf_op jit(solution)/shard_map/pallas_call | solution.py:257
  123.9 0.8 copy-done.9
  124.8 4.5 %shard_map.48.refs_0_ = bf16[1536,2048]{1,0:T(8,128)(2,1)} custom-call(s32[4]{0:T(128)} %pad_add_fusion.at_ref, bf16[192,2048]{1,0:T(8,128)(2,1)} %bitcast.20, bf16[192,2048]{1,0:T(8,128)(2,1)} %bitcast.22, bf16[192,2048]{1,0:T(8,128)(2,1)} %bitcast.24, bf16[192,2048]{1,0:T(8,128)(2,1)} %copy-done.9, bf16[192,2048]{1,0:T(8,128)(2,1)} %collective-permute-done.3.refs_4_, ...), custom_call_target="tpu_custom_call" | custom-call | bytes 9437184 | tf_op jit(solution)/shard_map/pallas_call | solution.py:211
  129.3 2.6 %shard_map.49 = bf16[1536,2048]{1,0:T(8,128)(2,1)} custom-call(s32[4]{0:T(128)} %pad_add_fusion.at_ref, bf16[1536,2048]{1,0:T(8,128)(2,1)} %shard_map.48.refs_0_, bf16[96,2048]{1,0:T(8,128)(2,1)} %bitcast.28, bf16[96,2048]{1,0:T(8,128)(2,1)} %bitcast.12.refs_2_, bf16[96,2048]{1,0:T(8,128)(2,1)} %collective-permute-done.7.refs_3_, ...), custom_call_target="tpu_custom_call", output_to_operand_aliasing={{}: (1, {})} | custom-call | bytes 3145728 | tf_op jit(solution)/shard_map/pallas_call | solution.py:219
  132.0 4.9 %fusion.2 = f32[384,1536]{1,0:T(8,128)S(1)} fusion(bf16[1536,384]{1,0:T(8,128)(2,1)} %bitcast.2, bf16[1536,2048]{1,0:T(8,128)(2,1)} %shard_map.49), kind=kOutput, calls=%fused_computation.2 | convolution fusion | flops 1811939328 | bytes 8257536 | tf_op jit(solution)/shard_map/dot_general | solution.py:230
  136.9 2.2 %fusion.11 = bf16[384,512]{1,0:T(8,128)(2,1)S(1)} fusion(bf16[1536,384]{1,0:T(8,128)(2,1)} %bitcast.2, bf16[1536,2048]{1,0:T(8,128)(2,1)S(1)} %copy-done), kind=kOutput, calls=%fused_computation.10 | convolution fusion | flops 604176384 | bytes 3145728 | tf_op jit(solution)/shard_map/dot_general | solution.py:230
  139.1 1.0 fusion.8
  140.1 2.7 %fusion = f32[512,1536]{1,0:T(8,128)S(1)} fusion(bf16[1536,512]{1,0:T(8,128)(2,1)S(1)} %bitcast.26, bf16[1536,2048]{1,0:T(8,128)(2,1)S(1)} %copy-done), kind=kOutput, calls=%fused_computation | convolution fusion | flops 2415919104 | bytes 9437184 | tf_op jit(solution)/shard_map/dot_general | solution.py:230
  142.8 2.8 %collective-permute-start.11 = (bf16[192,512]{1,0:T(8,128)(2,1)S(1)}, bf16[192,512]{1,0:T(8,128)(2,1)S(1)}, u32[]{:S(2)}, u32[]{:S(2)}) collective-permute-start(bf16[192,512]{1,0:T(8,128)(2,1)S(1)} %get-tuple-element.36), channel_id=1, source_target_pairs={{0,192},{64,0},{128,64},{192,128},{1,193},{65,1},{129,65},{193,129... | collective-permute-start | bytes 589832 | tf_op jit(solution)/shard_map/ppermute | solution.py:137
  145.7 1.1 collective-permute-start.24
  146.7 2.6 %collective-permute-start.26 = (bf16[256,512]{1,0:T(8,128)(2,1)S(1)}, bf16[256,512]{1,0:T(8,128)(2,1)S(1)}, u32[]{:S(2)}, u32[]{:S(2)}) collective-permute-start(bf16[256,512]{1,0:T(8,128)(2,1)S(1)} %get-tuple-element.34), channel_id=1, source_target_pairs={{0,192},{64,0},{128,64},{192,128},{1,193},{65,1},{129,65},{193,129... | collective-permute-start | bytes 786440 | tf_op jit(solution)/shard_map/ppermute | solution.py:137
  149.3 1.6 collective-permute-done.11
  150.9 3.7 %collective-permute-done.9 = bf16[192,512]{1,0:T(8,128)(2,1)S(1)} collective-permute-done((bf16[192,512]{1,0:T(8,128)(2,1)S(1)}, bf16[192,512]{1,0:T(8,128)(2,1)S(1)}, u32[]{:S(2)}, u32[]{:S(2)}) %collective-permute-start.9) | collective-permute-done | bytes 196640 | tf_op jit(solution)/shard_map/ppermute | solution.py:137
  154.9 3.2 %collective-permute-start.12 = (bf16[384,512]{1,0:T(8,128)(2,1)S(1)}, bf16[384,512]{1,0:T(8,128)(2,1)S(1)}, u32[]{:S(2)}, u32[]{:S(2)}) collective-permute-start(bf16[384,512]{1,0:T(8,128)(2,1)S(1)} %get-tuple-element.32), channel_id=1, source_target_pairs={{0,192},{64,0},{128,64},{192,128},{1,193},{65,1},{129,65},{193,129... | collective-permute-start | bytes 1179656 | tf_op jit(solution)/shard_map/ppermute | solution.py:137
  158.1 2.1 %collective-permute-done.24 = bf16[256,512]{1,0:T(8,128)(2,1)S(1)} collective-permute-done((bf16[256,512]{1,0:T(8,128)(2,1)S(1)}, bf16[256,512]{1,0:T(8,128)(2,1)S(1)}, u32[]{:S(2)}, u32[]{:S(2)}) %collective-permute-start.24) | collective-permute-done | bytes 262176 | tf_op jit(solution)/shard_map/ppermute | solution.py:137
  160.6 3.2 %collective-permute-start.27 = (bf16[512,512]{1,0:T(8,128)(2,1)S(1)}, bf16[512,512]{1,0:T(8,128)(2,1)S(1)}, u32[]{:S(2)}, u32[]{:S(2)}) collective-permute-start(bf16[512,512]{1,0:T(8,128)(2,1)S(1)} %get-tuple-element.30), channel_id=1, source_target_pairs={{0,192},{64,0},{128,64},{192,128},{1,193},{65,1},{129,65},{193,129... | collective-permute-start | bytes 1572872 | tf_op jit(solution)/shard_map/ppermute | solution.py:137
  163.8 4.9 %collective-permute-done.10 = bf16[384,512]{1,0:T(8,128)(2,1)S(1)} collective-permute-done((bf16[384,512]{1,0:T(8,128)(2,1)S(1)}, bf16[384,512]{1,0:T(8,128)(2,1)S(1)}, u32[]{:S(2)}, u32[]{:S(2)}) %collective-permute-start.10) | collective-permute-done | bytes 393248 | tf_op jit(solution)/shard_map/ppermute | solution.py:137
  168.8 10.2 %collective-permute-done.25 = bf16[512,512]{1,0:T(8,128)(2,1)S(1)} collective-permute-done((bf16[512,512]{1,0:T(8,128)(2,1)S(1)}, bf16[512,512]{1,0:T(8,128)(2,1)S(1)}, u32[]{:S(2)}, u32[]{:S(2)}) %collective-permute-start.25) | collective-permute-done | bytes 524320 | tf_op jit(solution)/shard_map/ppermute | solution.py:137
  179.3 1.4 pad_maximum_fusion
  (70 shorter events, 4.4 us)
Async XLA Ops:
  2.3 30.2 %all-to-all-start.1 = ((bf16[8,24,2048]{2,1,0:T(8,128)(2,1)}), bf16[8,24,2048]{2,1,0:T(8,128)(2,1)S(1)}, u32[]{:S(2)}, u32[]{:S(2)}) async-start(bf16[8,24,2048]{2,1,0:T(8,128)(2,1)} %shard_map.47), calls=%async_computation.1 | async-start | bytes 1572864 | tf_op jit(solution)/shard_map/all_to_all | solution.py:159
  17.6 21.5 %collective-permute-start.13 = (bf16[2,8,24,512]{3,2,1,0:T(8,128)(2,1)}, bf16[2,8,24,512]{3,2,1,0:T(8,128)(2,1)S(1)}, u32[]{:S(2)}, u32[]{:S(2)}) collective-permute-start(bf16[2,8,24,512]{3,2,1,0:T(8,128)(2,1)} %get-tuple-element.18), channel_id=1, source_target_pairs={{0,2},{2,4},{4,6},{6,0},{1,3},{3,5},{5,7},{7,1},{8,10},{10,12},{12... | collective-permute-start | bytes 1179656 | tf_op jit(solution)/shard_map/ppermute | solution.py:137
  19.2 19.9 %collective-permute-start.14 = (bf16[2,8,24,512]{3,2,1,0:T(8,128)(2,1)}, bf16[2,8,24,512]{3,2,1,0:T(8,128)(2,1)S(1)}, u32[]{:S(2)}, u32[]{:S(2)}) collective-permute-start(bf16[2,8,24,512]{3,2,1,0:T(8,128)(2,1)} %get-tuple-element.19), channel_id=1, source_target_pairs={{0,4},{2,6},{4,0},{6,2},{1,5},{3,7},{5,1},{7,3},{8,12},{10,14},{12... | collective-permute-start | bytes 1179656 | tf_op jit(solution)/shard_map/ppermute | solution.py:137
  20.1 19.0 %collective-permute-start.15 = (bf16[2,8,24,512]{3,2,1,0:T(8,128)(2,1)}, bf16[2,8,24,512]{3,2,1,0:T(8,128)(2,1)S(1)}, u32[]{:S(2)}, u32[]{:S(2)}) collective-permute-start(bf16[2,8,24,512]{3,2,1,0:T(8,128)(2,1)} %get-tuple-element.20), channel_id=1, source_target_pairs={{0,6},{2,0},{4,2},{6,4},{1,7},{3,1},{5,3},{7,5},{8,14},{10,8},{12,... | collective-permute-start | bytes 1179656 | tf_op jit(solution)/shard_map/ppermute | solution.py:137
  32.6 59.2 %copy-start.1 = (bf16[8,24,2048]{2,1,0:T(8,128)(2,1)}, bf16[8,24,2048]{2,1,0:T(8,128)(2,1)S(1)}, u32[]{:S(2)}) copy-start(bf16[8,24,2048]{2,1,0:T(8,128)(2,1)S(1)} %all-to-all-done.1) | copy-start | bytes 2359300
  32.6 99.4 %all-to-all-start = ((bf16[64,24,384]{2,1,0:T(8,128)(2,1)}), bf16[64,24,384]{2,1,0:T(8,128)(2,1)}, u32[]{:S(2)}, u32[]{:S(2)}) async-start(bf16[64,24,384]{2,1,0:T(8,128)(2,1)} %bitcast.18), calls=%async_computation | async-start | bytes 2359296 | tf_op jit(solution)/shard_map/all_to_all | solution.py:196
  39.1 0.8 copy-start.4
  39.1 0.9 copy-start.5
  39.2 1.0 copy-start.6
  42.3 2.5 %collective-permute-start.16 = (bf16[4,8,24,512]{3,2,1,0:T(8,128)(2,1)}, bf16[4,8,24,512]{3,2,1,0:T(8,128)(2,1)S(1)}, u32[]{:S(2)}, u32[]{:S(2)}) collective-permute-start(bf16[4,8,24,512]{3,2,1,0:T(8,128)(2,1)} %shard_map.51), channel_id=1, source_target_pairs={{0,1},{1,0},{2,3},{3,2},{4,5},{5,4},{6,7},{7,6},{8,9},{9,8},{10,11... | collective-permute-start | bytes 2359304 | tf_op jit(solution)/shard_map/ppermute | solution.py:141
  42.6 43.8 %collective-permute-start = (bf16[8,24,2048]{2,1,0:T(8,128)(2,1)S(1)}, bf16[8,24,2048]{2,1,0:T(8,128)(2,1)S(1)}, u32[]{:S(2)}, u32[]{:S(2)}) collective-permute-start(bf16[8,24,2048]{2,1,0:T(8,128)(2,1)S(1)} %all-to-all-done.1), channel_id=1, source_target_pairs={{0,2},{2,4},{4,6},{6,0},{1,3},{3,5},{5,7},{7,1},{8,10},{10,12},{12... | collective-permute-start | bytes 2359304 | tf_op jit(solution)/shard_map/ppermute | solution.py:137
  44.1 43.2 %collective-permute-start.1 = (bf16[8,24,2048]{2,1,0:T(8,128)(2,1)S(1)}, bf16[8,24,2048]{2,1,0:T(8,128)(2,1)S(1)}, u32[]{:S(2)}, u32[]{:S(2)}) collective-permute-start(bf16[8,24,2048]{2,1,0:T(8,128)(2,1)S(1)} %all-to-all-done.1), channel_id=1, source_target_pairs={{0,6},{2,0},{4,2},{6,4},{1,7},{3,1},{5,3},{7,5},{8,14},{10,8},{12,... | collective-permute-start | bytes 2359304 | tf_op jit(solution)/shard_map/ppermute | solution.py:137
  44.8 0.9 copy-start.8
  48.4 22.0 %collective-permute-start.17 = (bf16[8,24,512]{2,1,0:T(8,128)(2,1)}, bf16[8,24,512]{2,1,0:T(8,128)(2,1)S(1)}, u32[]{:S(2)}, u32[]{:S(2)}) collective-permute-start(bf16[8,24,512]{2,1,0:T(8,128)(2,1)} %get-tuple-element.22), channel_id=1, source_target_pairs={{0,8},{8,16},{16,24},{24,32},{32,40},{40,48},{48,56},{56,0},{1,9},... | collective-permute-start | bytes 589832 | tf_op jit(solution)/shard_map/ppermute | solution.py:137
  49.8 31.9 %collective-permute-start.18 = (bf16[8,24,512]{2,1,0:T(8,128)(2,1)}, bf16[8,24,512]{2,1,0:T(8,128)(2,1)S(1)}, u32[]{:S(2)}, u32[]{:S(2)}) collective-permute-start(bf16[8,24,512]{2,1,0:T(8,128)(2,1)} %get-tuple-element.23), channel_id=1, source_target_pairs={{0,16},{8,24},{16,32},{24,40},{32,48},{40,56},{48,0},{56,8},{1,17}... | collective-permute-start | bytes 589832 | tf_op jit(solution)/shard_map/ppermute | solution.py:137
  53.4 38.3 %collective-permute-start.19 = (bf16[8,24,512]{2,1,0:T(8,128)(2,1)}, bf16[8,24,512]{2,1,0:T(8,128)(2,1)S(1)}, u32[]{:S(2)}, u32[]{:S(2)}) collective-permute-start(bf16[8,24,512]{2,1,0:T(8,128)(2,1)} %get-tuple-element.24), channel_id=1, source_target_pairs={{0,24},{8,32},{16,40},{24,48},{32,56},{40,0},{48,8},{56,16},{1,25}... | collective-permute-start | bytes 589832 | tf_op jit(solution)/shard_map/ppermute | solution.py:137
  70.4 16.9 %copy-start.11 = (bf16[8,24,512]{2,1,0:T(8,128)(2,1)}, bf16[8,24,512]{2,1,0:T(8,128)(2,1)S(1)}, u32[]{:S(2)}) copy-start(bf16[8,24,512]{2,1,0:T(8,128)(2,1)S(1)} %collective-permute-done.17.refs_1_) | copy-start | bytes 589828
  70.4 21.4 %collective-permute-start.20 = (bf16[8,24,512]{2,1,0:T(8,128)(2,1)}, bf16[8,24,512]{2,1,0:T(8,128)(2,1)S(1)}, u32[]{:S(2)}, u32[]{:S(2)}) collective-permute-start(bf16[8,24,512]{2,1,0:T(8,128)(2,1)} %get-tuple-element.25), channel_id=1, source_target_pairs={{0,32},{8,40},{16,48},{24,56},{32,0},{40,8},{48,16},{56,24},{1,33}... | collective-permute-start | bytes 589832 | tf_op jit(solution)/shard_map/ppermute | solution.py:137
  81.7 5.6 %copy-start.12 = (bf16[8,24,512]{2,1,0:T(8,128)(2,1)}, bf16[8,24,512]{2,1,0:T(8,128)(2,1)S(1)}, u32[]{:S(2)}) copy-start(bf16[8,24,512]{2,1,0:T(8,128)(2,1)S(1)} %collective-permute-done.18.refs_2_) | copy-start | bytes 589828
  81.7 21.6 %collective-permute-start.21 = (bf16[8,24,512]{2,1,0:T(8,128)(2,1)}, bf16[8,24,512]{2,1,0:T(8,128)(2,1)S(1)}, u32[]{:S(2)}, u32[]{:S(2)}) collective-permute-start(bf16[8,24,512]{2,1,0:T(8,128)(2,1)} %get-tuple-element.26), channel_id=1, source_target_pairs={{0,40},{8,48},{16,56},{24,0},{32,8},{40,16},{48,24},{56,32},{1,41}... | collective-permute-start | bytes 589832 | tf_op jit(solution)/shard_map/ppermute | solution.py:137
  86.4 37.5 %copy-start.2 = (bf16[8,24,2048]{2,1,0:T(8,128)(2,1)}, bf16[8,24,2048]{2,1,0:T(8,128)(2,1)S(1)}, u32[]{:S(2)}) copy-start(bf16[8,24,2048]{2,1,0:T(8,128)(2,1)S(1)} %collective-permute-done) | copy-start | bytes 2359300
  86.4 19.5 %collective-permute-start.22 = (bf16[8,24,512]{2,1,0:T(8,128)(2,1)}, bf16[8,24,512]{2,1,0:T(8,128)(2,1)S(1)}, u32[]{:S(2)}, u32[]{:S(2)}) collective-permute-start(bf16[8,24,512]{2,1,0:T(8,128)(2,1)} %get-tuple-element.27), channel_id=1, source_target_pairs={{0,48},{8,56},{16,0},{24,8},{32,16},{40,24},{48,32},{56,40},{1,49}... | collective-permute-start | bytes 589832 | tf_op jit(solution)/shard_map/ppermute | solution.py:137
  87.3 36.6 %copy-start.3 = (bf16[8,24,2048]{2,1,0:T(8,128)(2,1)}, bf16[8,24,2048]{2,1,0:T(8,128)(2,1)S(1)}, u32[]{:S(2)}) copy-start(bf16[8,24,2048]{2,1,0:T(8,128)(2,1)S(1)} %collective-permute-done.1) | copy-start | bytes 2359300
  87.3 23.0 %collective-permute-start.23 = (bf16[8,24,512]{2,1,0:T(8,128)(2,1)}, bf16[8,24,512]{2,1,0:T(8,128)(2,1)S(1)}, u32[]{:S(2)}, u32[]{:S(2)}) collective-permute-start(bf16[8,24,512]{2,1,0:T(8,128)(2,1)} %get-tuple-element.28), channel_id=1, source_target_pairs={{0,56},{8,0},{16,8},{24,16},{32,24},{40,32},{48,40},{56,48},{1,57}... | collective-permute-start | bytes 589832 | tf_op jit(solution)/shard_map/ppermute | solution.py:137
  91.8 29.3 %copy-start.13 = (bf16[8,24,512]{2,1,0:T(8,128)(2,1)}, bf16[8,24,512]{2,1,0:T(8,128)(2,1)S(1)}, u32[]{:S(2)}) copy-start(bf16[8,24,512]{2,1,0:T(8,128)(2,1)S(1)} %collective-permute-done.19.refs_3_) | copy-start | bytes 589828
  91.8 32.1 %collective-permute-start.2 = (bf16[192,2048]{1,0:T(8,128)(2,1)S(1)}, bf16[192,2048]{1,0:T(8,128)(2,1)S(1)}, u32[]{:S(2)}, u32[]{:S(2)}) collective-permute-start(bf16[192,2048]{1,0:T(8,128)(2,1)S(1)} %bitcast.19), channel_id=1, source_target_pairs={{0,1},{1,0},{2,3},{3,2},{4,5},{5,4},{6,7},{7,6},{8,9},{9,8},{10,11... | collective-permute-start | bytes 2359304 | tf_op jit(solution)/shard_map/ppermute | solution.py:141
  91.8 29.3 %copy-start.14 = (bf16[8,24,512]{2,1,0:T(8,128)(2,1)}, bf16[8,24,512]{2,1,0:T(8,128)(2,1)S(1)}, u32[]{:S(2)}) copy-start(bf16[8,24,512]{2,1,0:T(8,128)(2,1)S(1)} %collective-permute-done.20.refs_4_) | copy-start | bytes 589828
  91.8 32.1 %collective-permute-start.3 = (bf16[192,2048]{1,0:T(8,128)(2,1)S(1)}, bf16[192,2048]{1,0:T(8,128)(2,1)}, u32[]{:S(2)}, u32[]{:S(2)}) collective-permute-start(bf16[192,2048]{1,0:T(8,128)(2,1)S(1)} %bitcast.21), channel_id=1, source_target_pairs={{0,1},{1,0},{2,3},{3,2},{4,5},{5,4},{6,7},{7,6},{8,9},{9,8},{10,11... | collective-permute-start | bytes 2359304 | tf_op jit(solution)/shard_map/ppermute | solution.py:141
  103.3 17.8 %copy-start.15 = (bf16[8,24,512]{2,1,0:T(8,128)(2,1)}, bf16[8,24,512]{2,1,0:T(8,128)(2,1)S(1)}, u32[]{:S(2)}) copy-start(bf16[8,24,512]{2,1,0:T(8,128)(2,1)S(1)} %collective-permute-done.21.refs_5_) | copy-start | bytes 589828
  103.3 10.2 %collective-permute-start.5 = (bf16[4,24,2048]{2,1,0:T(8,128)(2,1)S(1)}, bf16[4,24,2048]{2,1,0:T(8,128)(2,1)S(1)}, u32[]{:S(2)}, u32[]{:S(2)}) collective-permute-start(bf16[4,24,2048]{2,1,0:T(8,128)(2,1)S(1)} %slice.58), channel_id=1, source_target_pairs={{0,2},{2,4},{4,6},{6,0},{1,3},{3,5},{5,7},{7,1},{8,10},{10,12},{12... | collective-permute-start | bytes 1179656 | tf_op jit(solution)/shard_map/ppermute | solution.py:137
  105.9 15.2 %copy-start.16 = (bf16[8,24,512]{2,1,0:T(8,128)(2,1)}, bf16[8,24,512]{2,1,0:T(8,128)(2,1)S(1)}, u32[]{:S(2)}) copy-start(bf16[8,24,512]{2,1,0:T(8,128)(2,1)S(1)} %collective-permute-done.22.refs_6_) | copy-start | bytes 589828
  105.9 18.0 %collective-permute-start.4 = (bf16[192,2048]{1,0:T(8,128)(2,1)S(1)}, bf16[192,2048]{1,0:T(8,128)(2,1)}, u32[]{:S(2)}, u32[]{:S(2)}) collective-permute-start(bf16[192,2048]{1,0:T(8,128)(2,1)S(1)} %bitcast.23), channel_id=1, source_target_pairs={{0,1},{1,0},{2,3},{3,2},{4,5},{5,4},{6,7},{7,6},{8,9},{9,8},{10,11... | collective-permute-start | bytes 2359304 | tf_op jit(solution)/shard_map/ppermute | solution.py:141
  110.3 10.8 %copy-start.17 = (bf16[8,24,512]{2,1,0:T(8,128)(2,1)}, bf16[8,24,512]{2,1,0:T(8,128)(2,1)S(1)}, u32[]{:S(2)}) copy-start(bf16[8,24,512]{2,1,0:T(8,128)(2,1)S(1)} %collective-permute-done.23.refs_7_) | copy-start | bytes 589828
  110.3 10.8 %collective-permute-start.6 = (bf16[4,24,2048]{2,1,0:T(8,128)(2,1)S(1)}, bf16[4,24,2048]{2,1,0:T(8,128)(2,1)}, u32[]{:S(2)}, u32[]{:S(2)}) collective-permute-start(bf16[4,24,2048]{2,1,0:T(8,128)(2,1)S(1)} %slice.59), channel_id=1, source_target_pairs={{0,6},{2,0},{4,2},{6,4},{1,7},{3,1},{5,3},{7,5},{8,14},{10,8},{12,... | collective-permute-start | bytes 1179656 | tf_op jit(solution)/shard_map/ppermute | solution.py:137
  113.5 15.8 %copy-start.10 = (bf16[4,24,2048]{2,1,0:T(8,128)(2,1)}, bf16[4,24,2048]{2,1,0:T(8,128)(2,1)S(1)}, u32[]{:S(2)}) copy-start(bf16[4,24,2048]{2,1,0:T(8,128)(2,1)S(1)} %collective-permute-done.5) | copy-start | bytes 1179652
  113.5 15.8 %collective-permute-start.7 = (bf16[96,2048]{1,0:T(8,128)(2,1)S(1)}, bf16[96,2048]{1,0:T(8,128)(2,1)}, u32[]{:S(2)}, u32[]{:S(2)}) collective-permute-start(bf16[96,2048]{1,0:T(8,128)(2,1)S(1)} %bitcast.27), channel_id=1, source_target_pairs={{0,1},{1,0},{2,3},{3,2},{4,5},{5,4},{6,7},{7,6},{8,9},{9,8},{10,11... | collective-permute-start | bytes 1179656 | tf_op jit(solution)/shard_map/ppermute | solution.py:141
  121.1 8.3 %collective-permute-start.8 = (bf16[96,2048]{1,0:T(8,128)(2,1)}, bf16[96,2048]{1,0:T(8,128)(2,1)}, u32[]{:S(2)}, u32[]{:S(2)}) collective-permute-start(bf16[96,2048]{1,0:T(8,128)(2,1)} %bitcast.12.refs_2_), channel_id=1, source_target_pairs={{0,1},{1,0},{2,3},{3,2},{4,5},{5,4},{6,7},{7,6},{8,9},{9,8},{10,11... | collective-permute-start | bytes 1179656 | tf_op jit(solution)/shard_map/ppermute | solution.py:141
  123.9 0.9 copy-start.9
  132.0 4.9 %copy-start = (bf16[1536,2048]{1,0:T(8,128)(2,1)S(1)}, bf16[1536,2048]{1,0:T(8,128)(2,1)}, u32[]{:S(2)}) copy-start(bf16[1536,2048]{1,0:T(8,128)(2,1)} %shard_map.49) | copy-start | bytes 18874372
  136.8 2.2 %copy-start.7 = (bf16[64,24,512]{2,1,0:T(8,128)(2,1)S(1)}, bf16[64,24,512]{2,1,0:T(8,128)(2,1)}, u32[]{:S(2)}) copy-start(bf16[64,24,512]{2,1,0:T(8,128)(2,1)} %shard_map.53) | copy-start | bytes 4718596
  142.8 8.1 %collective-permute-start.11 = (bf16[192,512]{1,0:T(8,128)(2,1)S(1)}, bf16[192,512]{1,0:T(8,128)(2,1)S(1)}, u32[]{:S(2)}, u32[]{:S(2)}) collective-permute-start(bf16[192,512]{1,0:T(8,128)(2,1)S(1)} %get-tuple-element.36), channel_id=1, source_target_pairs={{0,192},{64,0},{128,64},{192,128},{1,193},{65,1},{129,65},{193,129... | collective-permute-start | bytes 589832 | tf_op jit(solution)/shard_map/ppermute | solution.py:137
  145.6 9.0 %collective-permute-start.9 = (bf16[192,512]{1,0:T(8,128)(2,1)S(1)}, bf16[192,512]{1,0:T(8,128)(2,1)S(1)}, u32[]{:S(2)}, u32[]{:S(2)}) collective-permute-start(bf16[192,512]{1,0:T(8,128)(2,1)S(1)} %get-tuple-element.35), channel_id=1, source_target_pairs={{0,64},{64,128},{128,192},{192,0},{1,65},{65,129},{129,193},{193,1... | collective-permute-start | bytes 589832 | tf_op jit(solution)/shard_map/ppermute | solution.py:137
  145.7 14.6 %collective-permute-start.24 = (bf16[256,512]{1,0:T(8,128)(2,1)S(1)}, bf16[256,512]{1,0:T(8,128)(2,1)S(1)}, u32[]{:S(2)}, u32[]{:S(2)}) collective-permute-start(bf16[256,512]{1,0:T(8,128)(2,1)S(1)} %get-tuple-element.33), channel_id=1, source_target_pairs={{0,64},{64,128},{128,192},{192,0},{1,65},{65,129},{129,193},{193,1... | collective-permute-start | bytes 786440 | tf_op jit(solution)/shard_map/ppermute | solution.py:137
  146.7 13.5 %collective-permute-start.26 = (bf16[256,512]{1,0:T(8,128)(2,1)S(1)}, bf16[256,512]{1,0:T(8,128)(2,1)S(1)}, u32[]{:S(2)}, u32[]{:S(2)}) collective-permute-start(bf16[256,512]{1,0:T(8,128)(2,1)S(1)} %get-tuple-element.34), channel_id=1, source_target_pairs={{0,192},{64,0},{128,64},{192,128},{1,193},{65,1},{129,65},{193,129... | collective-permute-start | bytes 786440 | tf_op jit(solution)/shard_map/ppermute | solution.py:137
  154.8 13.9 %collective-permute-start.10 = (bf16[384,512]{1,0:T(8,128)(2,1)S(1)}, bf16[384,512]{1,0:T(8,128)(2,1)S(1)}, u32[]{:S(2)}, u32[]{:S(2)}) collective-permute-start(bf16[384,512]{1,0:T(8,128)(2,1)S(1)} %get-tuple-element.31), channel_id=1, source_target_pairs={{0,64},{64,128},{128,192},{192,0},{1,65},{65,129},{129,193},{193,1... | collective-permute-start | bytes 1179656 | tf_op jit(solution)/shard_map/ppermute | solution.py:137
  154.9 13.8 %collective-permute-start.12 = (bf16[384,512]{1,0:T(8,128)(2,1)S(1)}, bf16[384,512]{1,0:T(8,128)(2,1)S(1)}, u32[]{:S(2)}, u32[]{:S(2)}) collective-permute-start(bf16[384,512]{1,0:T(8,128)(2,1)S(1)} %get-tuple-element.32), channel_id=1, source_target_pairs={{0,192},{64,0},{128,64},{192,128},{1,193},{65,1},{129,65},{193,129... | collective-permute-start | bytes 1179656 | tf_op jit(solution)/shard_map/ppermute | solution.py:137
  160.5 18.6 %collective-permute-start.25 = (bf16[512,512]{1,0:T(8,128)(2,1)S(1)}, bf16[512,512]{1,0:T(8,128)(2,1)S(1)}, u32[]{:S(2)}, u32[]{:S(2)}) collective-permute-start(bf16[512,512]{1,0:T(8,128)(2,1)S(1)} %get-tuple-element.29), channel_id=1, source_target_pairs={{0,64},{64,128},{128,192},{192,0},{1,65},{65,129},{129,193},{193,1... | collective-permute-start | bytes 1572872 | tf_op jit(solution)/shard_map/ppermute | solution.py:137
  160.6 18.5 %collective-permute-start.27 = (bf16[512,512]{1,0:T(8,128)(2,1)S(1)}, bf16[512,512]{1,0:T(8,128)(2,1)S(1)}, u32[]{:S(2)}, u32[]{:S(2)}) collective-permute-start(bf16[512,512]{1,0:T(8,128)(2,1)S(1)} %get-tuple-element.30), channel_id=1, source_target_pairs={{0,192},{64,0},{128,64},{192,128},{1,193},{65,1},{129,65},{193,129... | collective-permute-start | bytes 1572872 | tf_op jit(solution)/shard_map/ppermute | solution.py:137
